TPU v7x, 512 devices: a whole 4x8x8 slice. The times are simulated.
512 devices in a mesh: seq: 32 (over y, x), stretch: 16 (over z, core).
Axes of the slice: x: 4, y: 8, z: 8, core: 2. Of those that a mesh axis runs over, the one named last changes fastest.
Arguments:
- queries: bfloat16 [65536, 1792], P(('stretch', 'seq')), may hold values from -140 to 140
- keys: bfloat16 [65536, 256], P(('stretch', 'seq')), may hold values from -6 to 6
- values: bfloat16 [65536, 256], P(('stretch', 'seq')), may hold values from -6 to 6
Outputs:
- attended: bfloat16 [65536, 1792], P(('stretch', 'seq'))
All inputs are finite; a program needn't handle non-finite values.
Results may differ from a plain program's by a relative error of at most 0.011.
Values may be sent and summed in bfloat16 or wider, within the bound.
No kernel may reach another device: no remote copies, remote signals or barrier semaphores. Data moves between devices by JAX's collectives and lax.ppermute only.
A program may use at most 64 MiB of HBM per device.

v0:
```python
import functools
import math

import jax
import jax.numpy as jnp
from jax import lax
from jax.experimental import pallas as pl
from jax.experimental.pallas import tpu as pltpu
from jax.sharding import PartitionSpec as P

QUERY_HEADS = 14
KEY_VALUE_HEADS = 2
HEAD_SIZE = 128
BLOCKS = 4
GROUP = QUERY_HEADS // KEY_VALUE_HEADS
ROWS = 128
STACKED = GROUP * ROWS
X = 4
Y = 8
SPAN = X * ROWS
EXPONENT = math.log2(math.e) / math.sqrt(HEAD_SIZE)
LOWEST = -1e30
CHUNK = 896


def worker(sequence, head, core):
    plane = 4 * (sequence % 2) + 2 * head + 1 - sequence // 2
    return 2 * plane + core


def stretch_pairs(which):
    pairs = []
    for sequence in range(4):
        for block in range(BLOCKS):
            head = (0 if block < 2 else 1) ^ which
            core = 0 if block in (0, 3) else 1
            pairs.append((4 * block + sequence, worker(sequence, head, core)))
    return pairs


def back(pairs):
    return [(b, a) for a, b in pairs]


def plane_shift(dx, dy):
    pairs = []
    for y in range(Y):
        for x in range(X):
            for g in range(16):
                target = ((y + dy) % Y) * X + (x + dx) % X
                pairs.append(((y * X + x) * 16 + g, target * 16 + g))
    return pairs


SWAP = [(i, i ^ 1) for i in range(16)]


def shifted(array, dx, dy):
    return lax.ppermute(array, ("seq", "stretch"), plane_shift(dx, dy))


def tables(positions):
    half = HEAD_SIZE // 2
    lane = jnp.arange(HEAD_SIZE, dtype=jnp.int32)
    inverse = 10000000.0 ** (-((lane % half).astype(jnp.float32) * 2.0) / HEAD_SIZE)
    angles = positions.astype(jnp.float32)[..., None] * inverse
    return jnp.cos(angles), jnp.where(lane < half, -jnp.sin(angles), jnp.sin(angles))


def spin(x, cosine, sine):
    return x * cosine + pltpu.roll(x, HEAD_SIZE // 2, 1) * sine


VMEM = pl.BlockSpec(memory_space=pltpu.VMEM)
SMEM = pl.BlockSpec(memory_space=pltpu.SMEM)


def unpack_kernel(where_ref, one_ref, two_ref, cosine_ref, sine_ref, out_ref, raw_ref):
    head = where_ref[0]
    cosine = cosine_ref[0]
    sine = sine_ref[0]
    for k, ref in enumerate((one_ref, two_ref)):
        slot = head ^ k
        place = pl.multiple_of(slot * (2 * HEAD_SIZE), 2 * HEAD_SIZE)
        x = ref[:, :HEAD_SIZE].astype(jnp.float32)
        out_ref[:, pl.ds(place, HEAD_SIZE)] = spin(x, cosine, sine).astype(jnp.bfloat16)
        out_ref[:, pl.ds(place + HEAD_SIZE, HEAD_SIZE)] = ref[:, HEAD_SIZE : 2 * HEAD_SIZE]
        raw_ref[slot] = ref[:, 2 * HEAD_SIZE :]


def query_kernel(where_ref, own_ref, other_ref, cosine_ref, sine_ref, out_ref):
    core = where_ref[1]

    def turn(ref, which, kind, slot):
        cosine = cosine_ref[kind]
        sine = sine_ref[kind]
        for g in range(GROUP):
            x = ref[which, :, g * HEAD_SIZE : (g + 1) * HEAD_SIZE].astype(jnp.float32)
            out_ref[slot, g * ROWS : (g + 1) * ROWS, :] = spin(x, cosine, sine).astype(jnp.bfloat16)

    turn(own_ref, 0, 0, 0)
    turn(own_ref, 1, 0, 1)
    turn(other_ref, 1, 2, 3)

    @pl.when(core == 0)
    def _():
        turn(other_ref, 0, 1, 2)
        turn(own_ref, 1, 2, 4)

    @pl.when(core == 1)
    def _():
        turn(own_ref, 1, 1, 2)
        turn(other_ref, 1, 1, 4)


def lanes(x, count):
    return [x[:, j * HEAD_SIZE : (j + 1) * HEAD_SIZE] for j in range(count)]


def absorb(query_ref, query, pairs, acc_ref, top_ref, sum_ref, slot, limit):
    def score(c):
        part = query_ref[query, c * CHUNK : (c + 1) * CHUNK, :]
        return [
            lax.dot_general(
                part, keys, (((1,), (1,)), ((), ())), preferred_element_type=jnp.float32
            )
            for keys, _ in pairs
        ]

    steps = STACKED // CHUNK
    coming = score(0)
    for c in range(steps):
        scores = coming
        if c + 1 < steps:
            coming = score(c + 1)
        if limit is not None:
            row = lax.broadcasted_iota(jnp.int32, (CHUNK, SPAN), 0) + c * CHUNK
            inside = limit[0] <= (row & (ROWS - 1)) + limit[1]
            scores = [jnp.where(inside, s, LOWEST) for s in scores]
        rows = pl.ds(c * CHUNK, CHUNK)
        parts = [part for s in scores for part in lanes(s, s.shape[1] // HEAD_SIZE)]
        highest = parts[0]
        for j in range(1, len(parts)):
            highest = jnp.maximum(highest, parts[j])
        before = top_ref[slot, rows, :]
        top = jnp.maximum(before, jnp.max(highest, axis=-1, keepdims=True))
        scaled = top * EXPONENT
        weights = [jnp.exp2(part * EXPONENT - scaled) for part in parts]
        fade = jnp.exp2(before * EXPONENT - scaled)
        total = weights[0]
        for j in range(1, len(parts)):
            total = total + weights[j]
        product = None
        used = 0
        for _, values in pairs:
            count = values.shape[0] // HEAD_SIZE
            some = weights[used : used + count]
            used += count
            packed = jnp.concatenate([w.astype(jnp.bfloat16) for w in some], axis=1)
            more = jnp.dot(packed, values, preferred_element_type=jnp.float32)
            product = more if product is None else product + more
        top_ref[slot, rows, :] = top
        sum_ref[slot, rows, :] = sum_ref[slot, rows, :] * fade + total
        acc_ref[slot, rows, :] = acc_ref[slot, rows, :] * fade + product


def attend_kernel(first, last, offsets, where_ref, query_ref, *refs):
    number = len(offsets)
    block_refs = refs[:number]
    refs = refs[number:]
    if last:
        out_refs = refs[3:5]
        refs = refs[:3] + refs[5:]
    if not first:
        for source, target in zip(refs[:3], refs[3:6]):
            target[...] = source[...]
        refs = refs[3:]
    acc_ref, top_ref, sum_ref = refs[:3]
    core = where_ref[1]
    x = where_ref[2]
    y = where_ref[3]
    if first:
        acc_ref[...] = jnp.zeros_like(acc_ref)
        top_ref[...] = jnp.full_like(top_ref, LOWEST)
        sum_ref[...] = jnp.zeros_like(sum_ref)
    run = functools.partial(
        absorb, query_ref, acc_ref=acc_ref, top_ref=top_ref, sum_ref=sum_ref
    )

    def columns(ref, place):
        keys = ref[:, pl.ds(place, HEAD_SIZE)]
        values = ref[:, pl.ds(place + HEAD_SIZE, HEAD_SIZE)]
        return keys, values

    def causal(ref, limit):
        def body(query, carry):
            place = pl.multiple_of(query * (2 * HEAD_SIZE), 2 * HEAD_SIZE)
            run(query=query, pairs=[columns(ref, place)], slot=query, limit=limit)
            return carry

        lax.fori_loop(0, 2, body, 0)

    third = pl.multiple_of(core * (2 * HEAD_SIZE), 2 * HEAD_SIZE)
    pairs = [columns(ref, 0) for ref in block_refs]
    run(query=2, pairs=pairs, slot=2 - core, limit=None)
    run(query=3, pairs=pairs, slot=3, limit=None)
    pairs = [columns(ref, third) for ref in block_refs]
    run(query=4, pairs=pairs, slot=1 + 2 * core, limit=None)
    if first:
        column = lax.broadcasted_iota(jnp.int32, (CHUNK, SPAN), 1)
        causal(block_refs[0], (column, x * ROWS))
    else:
        for b in range(number):

            @pl.when(((y + offsets[b]) & (Y - 1)) < y)
            def _(b=b):
                causal(block_refs[b], None)

    if last:
        lane = lax.broadcasted_iota(jnp.int32, (STACKED, HEAD_SIZE), 1)
        for k in range(4):
            ref = out_refs[k // 2]
            total = jnp.sum(sum_ref[k], axis=-1, keepdims=True)
            ref[k % 2, :, :HEAD_SIZE] = acc_ref[k]
            ref[k % 2, :, HEAD_SIZE:] = jnp.where(lane < HEAD_SIZE // 2, top_ref[k], total)


def attend(where, query, blocks, offsets, state, first=False, last=False):
    number = len(blocks)
    block = jax.ShapeDtypeStruct((4, STACKED, HEAD_SIZE), jnp.float32)
    outs = [block] * 3
    if last:
        outs = [jax.ShapeDtypeStruct((2, STACKED, 2 * HEAD_SIZE), jnp.float32)] * 2
    flops = number * 4 * 4 * STACKED * SPAN * HEAD_SIZE
    return pl.pallas_call(
        functools.partial(attend_kernel, first, last, offsets),
        out_shape=outs,
        in_specs=[SMEM] + [VMEM] * (1 + number + len(state)),
        out_specs=[VMEM] * len(outs),
        scratch_shapes=[pltpu.VMEM(block.shape, block.dtype)] * 3 if last else [],
        cost_estimate=pl.CostEstimate(
            flops=flops, bytes_accessed=4 << 20, transcendentals=number * 4 * STACKED * SPAN
        ),
        compiler_params=pltpu.CompilerParams(vmem_limit_bytes=24 << 20),
        name="attend",
    )(where, query, *blocks, *state)


def halves(stats):
    lane = lax.broadcasted_iota(jnp.int32, stats.shape, 1)
    turned = pltpu.roll(stats, HEAD_SIZE // 2, 1)
    left = lane < HEAD_SIZE // 2
    return jnp.where(left, stats, turned), jnp.where(left, turned, stats)


def merge_kernel(where_ref, own_ref, other_ref, out_ref):
    head = where_ref[0]
    for k in range(2):
        place = head if k == 0 else 1 - head
        for g in range(GROUP):
            rows = slice(g * ROWS, (g + 1) * ROWS)
            top, own_sum = halves(own_ref[k, rows, HEAD_SIZE:])
            other_top, other_sum = halves(other_ref[k, rows, HEAD_SIZE:])
            highest = jnp.maximum(top, other_top)
            mine = jnp.exp2((top - highest) * EXPONENT)
            theirs = jnp.exp2((other_top - highest) * EXPONENT)
            total = own_sum * mine + other_sum * theirs
            value = own_ref[k, rows, :HEAD_SIZE] * mine + other_ref[k, rows, :HEAD_SIZE] * theirs
            out_ref[place, :, g * HEAD_SIZE : (g + 1) * HEAD_SIZE] = (value / total).astype(
                jnp.bfloat16
            )


def on_device(queries, keys, values):
    seq = lax.axis_index("seq")
    stretch = lax.axis_index("stretch")
    x = seq % X
    y = seq // X
    home_block = stretch // 4
    low = home_block < 2
    core = stretch % 2
    head = (stretch // 4) % 2
    positions = seq * ROWS + jnp.arange(ROWS, dtype=jnp.int32)
    length = ROWS * X * Y
    kind = jnp.arange(3, dtype=jnp.int32)[:, None]
    every = jnp.where(kind == 2, 2 * length - 1, positions[None, :] + kind * length)
    cosine, sine = tables(every)
    base = jnp.stack([head, core, x, y]).astype(jnp.int32)
    straight, crossed = stretch_pairs(0), stretch_pairs(1)

    half = GROUP * HEAD_SIZE
    packs = [
        jnp.concatenate(
            [
                keys[:, k * HEAD_SIZE : (k + 1) * HEAD_SIZE],
                values[:, k * HEAD_SIZE : (k + 1) * HEAD_SIZE],
                queries[:, k * half : (k + 1) * half],
            ],
            axis=1,
        )
        for k in range(KEY_VALUE_HEADS)
    ]
    one = lax.ppermute(jnp.where(low, packs[0], packs[1]), "stretch", straight)
    two = lax.ppermute(jnp.where(low, packs[1], packs[0]), "stretch", crossed)
    own, raw = pl.pallas_call(
        unpack_kernel,
        out_shape=[
            jax.ShapeDtypeStruct((ROWS, 4 * HEAD_SIZE), jnp.bfloat16),
            jax.ShapeDtypeStruct((2, ROWS, half), jnp.bfloat16),
        ],
        in_specs=[SMEM] + [VMEM] * 4,
        out_specs=[VMEM] * 2,
        compiler_params=pltpu.CompilerParams(vmem_limit_bytes=8 << 20),
        name="unpack",
    )(base, one, two, cosine, sine)
    lines = [[X * line + k for k in range(X)] for line in range(Y)]
    row = lax.all_gather(own, "seq", axis=0, tiled=True, axis_index_groups=lines)
    row, raw = lax.optimization_barrier((row, raw))
    other_raw = lax.ppermute(raw, "stretch", SWAP)
    query = pl.pallas_call(
        query_kernel,
        out_shape=jax.ShapeDtypeStruct((5, STACKED, HEAD_SIZE), jnp.bfloat16),
        in_specs=[SMEM] + [VMEM] * 4,
        out_specs=VMEM,
        cost_estimate=pl.CostEstimate(flops=2 << 30, bytes_accessed=4 << 20, transcendentals=0),
        compiler_params=pltpu.CompilerParams(vmem_limit_bytes=12 << 20),
        name="turn_queries",
    )(base, raw, other_raw, cosine, sine)
    up, down = row, row
    blocks, offsets, state = [row], (0,), []
    for hop in range(1, Y // 2 + 1):
        if hop == Y // 2:
            up, down = up[: SPAN // 2], down[SPAN // 2 :]
        next_up = shifted(up, 0, 1)
        next_down = shifted(down, 0, -1)
        state = attend(base, query, blocks, offsets, state, first=hop == 1)
        up, _ = lax.optimization_barrier((next_up, state[2]))
        down, _ = lax.optimization_barrier((next_down, state[2]))
        blocks, offsets = [next_up, next_down], (-hop, hop)
    mine, send = attend(base, query, blocks, (4, 4), state, last=True)
    received = lax.ppermute(send, "stretch", SWAP)
    merged = pl.pallas_call(
        merge_kernel,
        out_shape=jax.ShapeDtypeStruct((2, ROWS, half), jnp.bfloat16),
        in_specs=[SMEM] + [VMEM] * 2,
        out_specs=VMEM,
        compiler_params=pltpu.CompilerParams(vmem_limit_bytes=12 << 20),
        name="merge",
    )(base, mine, received)
    one = lax.ppermute(merged[0], "stretch", back(straight))
    two = lax.ppermute(merged[1], "stretch", back(crossed))
    return jnp.concatenate([jnp.where(low, one, two), jnp.where(low, two, one)], axis=1)


def solution(mesh):
    placed = P(("stretch", "seq"), None)
    return jax.shard_map(
        on_device,
        mesh=mesh,
        in_specs=(placed, placed, placed),
        out_specs=placed,
        check_vma=False,
    )
```

profile of v0, /device:TPU:56, one launch (start us, length us, event | category | flops | bytes accessed | tf_op | source)
XLA Modules:
  0.0 141.8 jit_solution(17509838142114201286)
XLA Ops:
  0.0 1.1 fusion.5
  1.1 0.8 fusion.6
  2.0 4.3 %collective-permute-start = (bf16[128,1152]{1,0:T(8,128)(2,1)S(1)}, bf16[128,1152]{1,0:T(8,128)(2,1)S(1)}, u32[]{:S(2)}, u32[]{:S(2)}) collective-permute-start(bf16[128,1152]{1,0:T(8,128)(2,1)S(1)} %get-tuple-element.54), channel_id=1, source_target_pairs={{0,2},{4,3},{8,7},{12,6},{1,10},{5,11},{9,15},{13,14},{2,0},{6,1},... | collective-permute-start | bytes 884744 | tf_op jit(solution)/shard_map/ppermute | solution.py:303
  6.3 5.5 %collective-permute-start.1 = (bf16[128,1152]{1,0:T(8,128)(2,1)S(1)}, bf16[128,1152]{1,0:T(8,128)(2,1)S(1)}, u32[]{:S(2)}, u32[]{:S(2)}) collective-permute-start(bf16[128,1152]{1,0:T(8,128)(2,1)S(1)} %get-tuple-element.53), channel_id=1, source_target_pairs={{0,6},{4,7},{8,3},{12,2},{1,14},{5,15},{9,11},{13,10},{2,4},{6,5},... | collective-permute-start | bytes 884744 | tf_op jit(solution)/shard_map/ppermute | solution.py:304
  12.2 0.8 negate_select_fusion
  12.9 10.2 %collective-permute-done.1.two_ref = bf16[128,1152]{1,0:T(8,128)(2,1)S(1)} collective-permute-done((bf16[128,1152]{1,0:T(8,128)(2,1)S(1)}, bf16[128,1152]{1,0:T(8,128)(2,1)S(1)}, u32[]{:S(2)}, u32[]{:S(2)}) %collective-permute-start.1) | collective-permute-done | bytes 294944 | tf_op jit(solution)/shard_map/ppermute | solution.py:304
  23.1 0.6 unpack.1
  23.8 13.6 %all_gather.3.refs_0_ = bf16[512,512]{1,0:T(8,128)(2,1)S(1)} all-gather(bf16[128,512]{1,0:T(8,128)(2,1)S(1)} %get-tuple-element.29), channel_id=1, replica_groups={{0,16,32,48},{64,80,96,112},{128,144,160,176},{192,208,224,240},{256,27..., dimensions={0}, use_global_device_ids=true | all-gather | bytes 655360 | tf_op jit(solution)/shard_map/all_gather | solution.py:317
  37.4 3.6 %collective-permute-start.2 = (bf16[2,128,896]{2,1,0:T(8,128)(2,1)S(1)}, bf16[2,128,896]{2,1,0:T(8,128)(2,1)S(1)}, u32[]{:S(2)}, u32[]{:S(2)}) collective-permute-start(bf16[2,128,896]{2,1,0:T(8,128)(2,1)S(1)} %get-tuple-element.31.own_ref), channel_id=1, source_target_pairs={{0,1},{1,0},{2,3},{3,2},{4,5},{5,4},{6,7},{7,6},{8,9},{9,8},{10,11... | collective-permute-start | bytes 1376264 | tf_op jit(solution)/shard_map/ppermute | solution.py:319
  41.0 3.3 %collective-permute-start.5 = (bf16[512,512]{1,0:T(8,128)(2,1)S(1)}, bf16[512,512]{1,0:T(8,128)(2,1)S(1)}, u32[]{:S(2)}, u32[]{:S(2)}) collective-permute-start(bf16[512,512]{1,0:T(8,128)(2,1)S(1)} %all_gather.3.refs_0_), channel_id=1, source_target_pairs={{0,448},{1,449},{2,450},{3,451},{4,452},{5,453},{6,454},{7,455},{8... | collective-permute-start | bytes 1572872 | tf_op jit(solution)/shard_map/ppermute | solution.py:59
  44.3 3.8 %collective-permute-start.3 = (bf16[512,512]{1,0:T(8,128)(2,1)S(1)}, bf16[512,512]{1,0:T(8,128)(2,1)S(1)}, u32[]{:S(2)}, u32[]{:S(2)}) collective-permute-start(bf16[512,512]{1,0:T(8,128)(2,1)S(1)} %all_gather.3.refs_0_), channel_id=1, source_target_pairs={{0,64},{1,65},{2,66},{3,67},{4,68},{5,69},{6,70},{7,71},{8,72},{9,... | collective-permute-start | bytes 1572872 | tf_op jit(solution)/shard_map/ppermute | solution.py:59
  48.1 1.1 turn_queries.1.query_ref
  49.2 5.3 %attend.5 = (f32[4,896,128]{2,1,0:T(8,128)S(1)}, f32[4,896,128]{2,1,0:T(8,128)S(1)}, f32[4,896,128]{2,1,0:T(8,128)S(1)}) custom-call(s32[4]{0:T(128)S(1)} %pad_add_fusion.where_ref, bf16[5,896,128]{2,1,0:T(8,128)(2,1)S(1)} %turn_queries.1.query_ref, bf16[512,512]{1,0:T(8,128)(2,1)S(1)} %all_gather.3.refs_0_), custom_call_target="tpu_custom_call" | custom-call | flops 939524096 | bytes 4194304 | tf_op jit(solution)/shard_map/attend/pallas_call | solution.py:235
  54.5 3.4 %collective-permute-done.5.refs_1_ = bf16[512,512]{1,0:T(8,128)(2,1)S(1)} collective-permute-done((bf16[512,512]{1,0:T(8,128)(2,1)S(1)}, bf16[512,512]{1,0:T(8,128)(2,1)S(1)}, u32[]{:S(2)}, u32[]{:S(2)}) %collective-permute-start.5) | collective-permute-done | bytes 524320 | tf_op jit(solution)/shard_map/ppermute | solution.py:59
  58.0 2.0 %collective-permute-start.7 = (bf16[512,512]{1,0:T(8,128)(2,1)S(1)}, bf16[512,512]{1,0:T(8,128)(2,1)S(1)}, u32[]{:S(2)}, u32[]{:S(2)}) collective-permute-start(bf16[512,512]{1,0:T(8,128)(2,1)S(1)} %collective-permute-done.5.refs_1_), channel_id=1, source_target_pairs={{0,448},{1,449},{2,450},{3,451},{4,452},{5,453},{6,454},{7,455},{8... | collective-permute-start | bytes 1572872 | tf_op jit(solution)/shard_map/ppermute | solution.py:59
  60.0 5.0 %collective-permute-start.4 = (bf16[512,512]{1,0:T(8,128)(2,1)S(1)}, bf16[512,512]{1,0:T(8,128)(2,1)S(1)}, u32[]{:S(2)}, u32[]{:S(2)}) collective-permute-start(bf16[512,512]{1,0:T(8,128)(2,1)S(1)} %collective-permute-done.3.refs_0_), channel_id=1, source_target_pairs={{0,64},{1,65},{2,66},{3,67},{4,68},{5,69},{6,70},{7,71},{8,72},{9,... | collective-permute-start | bytes 1572872 | tf_op jit(solution)/shard_map/ppermute | solution.py:59
  65.0 9.2 %attend.6 = (f32[4,896,128]{2,1,0:T(8,128)S(1)}, f32[4,896,128]{2,1,0:T(8,128)S(1)}, f32[4,896,128]{2,1,0:T(8,128)S(1)}) custom-call(s32[4]{0:T(128)S(1)} %pad_add_fusion.where_ref, bf16[5,896,128]{2,1,0:T(8,128)(2,1)S(1)} %turn_queries.1.query_ref, bf16[512,512]{1,0:T(8,128)(2,1)S(1)} %collective-permute-done.3.refs_0_, ...), custom_call_target="tpu_custom_call" | custom-call | flops 1879048192 | bytes 4194304 | tf_op jit(solution)/shard_map/attend/pallas_call | solution.py:235
  74.2 1.9 %collective-permute-start.9 = (bf16[512,512]{1,0:T(8,128)(2,1)S(1)}, bf16[512,512]{1,0:T(8,128)(2,1)S(1)}, u32[]{:S(2)}, u32[]{:S(2)}) collective-permute-start(bf16[512,512]{1,0:T(8,128)(2,1)S(1)} %collective-permute-done.7.refs_1_), channel_id=1, source_target_pairs={{0,448},{1,449},{2,450},{3,451},{4,452},{5,453},{6,454},{7,455},{8... | collective-permute-start | bytes 1572872 | tf_op jit(solution)/shard_map/ppermute | solution.py:59
  76.2 5.1 %collective-permute-start.6 = (bf16[512,512]{1,0:T(8,128)(2,1)S(1)}, bf16[512,512]{1,0:T(8,128)(2,1)S(1)}, u32[]{:S(2)}, u32[]{:S(2)}) collective-permute-start(bf16[512,512]{1,0:T(8,128)(2,1)S(1)} %collective-permute-done.4.refs_0_), channel_id=1, source_target_pairs={{0,64},{1,65},{2,66},{3,67},{4,68},{5,69},{6,70},{7,71},{8,72},{9,... | collective-permute-start | bytes 1572872 | tf_op jit(solution)/shard_map/ppermute | solution.py:59
  81.3 9.0 %attend.7 = (f32[4,896,128]{2,1,0:T(8,128)S(1)}, f32[4,896,128]{2,1,0:T(8,128)S(1)}, f32[4,896,128]{2,1,0:T(8,128)S(1)}) custom-call(s32[4]{0:T(128)S(1)} %pad_add_fusion.where_ref, bf16[5,896,128]{2,1,0:T(8,128)(2,1)S(1)} %turn_queries.1.query_ref, bf16[512,512]{1,0:T(8,128)(2,1)S(1)} %collective-permute-done.4.refs_0_, ...), custom_call_target="tpu_custom_call" | custom-call | flops 1879048192 | bytes 4194304 | tf_op jit(solution)/shard_map/attend/pallas_call | solution.py:235
  90.3 1.9 %collective-permute-start.10 = (bf16[256,512]{1,0:T(8,128)(2,1)S(1)}, bf16[256,512]{1,0:T(8,128)(2,1)S(1)}, u32[]{:S(2)}, u32[]{:S(2)}) collective-permute-start(bf16[256,512]{1,0:T(8,128)(2,1)S(1)} %slice.37), channel_id=1, source_target_pairs={{0,448},{1,449},{2,450},{3,451},{4,452},{5,453},{6,454},{7,455},{8... | collective-permute-start | bytes 786440 | tf_op jit(solution)/shard_map/ppermute | solution.py:59
  92.3 5.4 %collective-permute-start.8 = (bf16[256,512]{1,0:T(8,128)(2,1)S(1)}, bf16[256,512]{1,0:T(8,128)(2,1)S(1)}, u32[]{:S(2)}, u32[]{:S(2)}) collective-permute-start(bf16[256,512]{1,0:T(8,128)(2,1)S(1)} %slice.36), channel_id=1, source_target_pairs={{0,64},{1,65},{2,66},{3,67},{4,68},{5,69},{6,70},{7,71},{8,72},{9,... | collective-permute-start | bytes 786440 | tf_op jit(solution)/shard_map/ppermute | solution.py:59
  97.7 9.0 %attend.8 = (f32[4,896,128]{2,1,0:T(8,128)S(1)}, f32[4,896,128]{2,1,0:T(8,128)S(1)}, f32[4,896,128]{2,1,0:T(8,128)S(1)}) custom-call(s32[4]{0:T(128)S(1)} %pad_add_fusion.where_ref, bf16[5,896,128]{2,1,0:T(8,128)(2,1)S(1)} %turn_queries.1.query_ref, bf16[512,512]{1,0:T(8,128)(2,1)S(1)} %collective-permute-done.6.refs_0_, ...), custom_call_target="tpu_custom_call" | custom-call | flops 1879048192 | bytes 4194304 | tf_op jit(solution)/shard_map/attend/pallas_call | solution.py:235
  106.7 6.3 %attend.9 = (f32[2,896,256]{2,1,0:T(8,128)S(1)}, f32[2,896,256]{2,1,0:T(8,128)S(1)}) custom-call(s32[4]{0:T(128)S(1)} %pad_add_fusion.where_ref, bf16[5,896,128]{2,1,0:T(8,128)(2,1)S(1)} %turn_queries.1.query_ref, bf16[256,512]{1,0:T(8,128)(2,1)S(1)} %collective-permute-done.8.refs_0_, bf16[256,512]{1,0:T(8,128)(2,1)S(1)} %collective-permute-done.10.refs_1_, ...), custom_call_target="tpu_custom_call" | custom-call | flops 1879048192 | bytes 4194304 | tf_op jit(solution)/shard_map/attend/pallas_call | solution.py:235
  113.0 1.9 %collective-permute-start.11 = (f32[2,896,256]{2,1,0:T(8,128)S(1)}, f32[2,896,256]{2,1,0:T(8,128)S(1)}, u32[]{:S(2)}, u32[]{:S(2)}) collective-permute-start(f32[2,896,256]{2,1,0:T(8,128)S(1)} %get-tuple-element.52), channel_id=1, source_target_pairs={{0,1},{1,0},{2,3},{3,2},{4,5},{5,4},{6,7},{7,6},{8,9},{9,8},{10,11... | collective-permute-start | bytes 5505032 | tf_op jit(solution)/shard_map/ppermute | solution.py:341
  114.9 3.8 %collective-permute-done.11.other_ref = f32[2,896,256]{2,1,0:T(8,128)S(1)} collective-permute-done((f32[2,896,256]{2,1,0:T(8,128)S(1)}, f32[2,896,256]{2,1,0:T(8,128)S(1)}, u32[]{:S(2)}, u32[]{:S(2)}) %collective-permute-start.11) | collective-permute-done | bytes 1835040 | tf_op jit(solution)/shard_map/ppermute | solution.py:341
  118.7 1.3 merge.1
  120.0 7.5 %collective-permute-start.12 = (bf16[128,896]{1,0:T(8,128)(2,1)S(1)}, bf16[128,896]{1,0:T(8,128)(2,1)S(1)}, u32[]{:S(2)}, u32[]{:S(2)}) collective-permute-start(bf16[128,896]{1,0:T(8,128)(2,1)S(1)} %get-tuple-element.57), channel_id=1, source_target_pairs={{2,0},{3,4},{7,8},{6,12},{10,1},{11,5},{15,9},{14,13},{0,2},{1,6},... | collective-permute-start | bytes 688136 | tf_op jit(solution)/shard_map/ppermute | solution.py:350
  127.5 1.9 %collective-permute-start.13 = (bf16[128,896]{1,0:T(8,128)(2,1)S(1)}, bf16[128,896]{1,0:T(8,128)(2,1)S(1)}, u32[]{:S(2)}, u32[]{:S(2)}) collective-permute-start(bf16[128,896]{1,0:T(8,128)(2,1)S(1)} %get-tuple-element.58), channel_id=1, source_target_pairs={{6,0},{7,4},{3,8},{2,12},{14,1},{15,5},{11,9},{10,13},{4,2},{5,6},... | collective-permute-start | bytes 688136 | tf_op jit(solution)/shard_map/ppermute | solution.py:351
  129.4 4.4 %collective-permute-done.12 = bf16[128,896]{1,0:T(8,128)(2,1)S(1)} collective-permute-done((bf16[128,896]{1,0:T(8,128)(2,1)S(1)}, bf16[128,896]{1,0:T(8,128)(2,1)S(1)}, u32[]{:S(2)}, u32[]{:S(2)}) %collective-permute-start.12) | collective-permute-done | bytes 229408 | tf_op jit(solution)/shard_map/ppermute | solution.py:350
  133.8 7.1 %collective-permute-done.13 = bf16[128,896]{1,0:T(8,128)(2,1)S(1)} collective-permute-done((bf16[128,896]{1,0:T(8,128)(2,1)S(1)}, bf16[128,896]{1,0:T(8,128)(2,1)S(1)}, u32[]{:S(2)}, u32[]{:S(2)}) %collective-permute-start.13) | collective-permute-done | bytes 229408 | tf_op jit(solution)/shard_map/ppermute | solution.py:351
  141.0 0.8 pad_maximum_fusion
  (21 shorter events, 0.4 us)
Async XLA Ops:
  2.0 10.9 %collective-permute-start = (bf16[128,1152]{1,0:T(8,128)(2,1)S(1)}, bf16[128,1152]{1,0:T(8,128)(2,1)S(1)}, u32[]{:S(2)}, u32[]{:S(2)}) collective-permute-start(bf16[128,1152]{1,0:T(8,128)(2,1)S(1)} %get-tuple-element.54), channel_id=1, source_target_pairs={{0,2},{4,3},{8,7},{12,6},{1,10},{5,11},{9,15},{13,14},{2,0},{6,1},... | collective-permute-start | bytes 884744 | tf_op jit(solution)/shard_map/ppermute | solution.py:303
  6.3 16.8 %collective-permute-start.1 = (bf16[128,1152]{1,0:T(8,128)(2,1)S(1)}, bf16[128,1152]{1,0:T(8,128)(2,1)S(1)}, u32[]{:S(2)}, u32[]{:S(2)}) collective-permute-start(bf16[128,1152]{1,0:T(8,128)(2,1)S(1)} %get-tuple-element.53), channel_id=1, source_target_pairs={{0,6},{4,7},{8,3},{12,2},{1,14},{5,15},{9,11},{13,10},{2,4},{6,5},... | collective-permute-start | bytes 884744 | tf_op jit(solution)/shard_map/ppermute | solution.py:304
  37.4 10.7 %collective-permute-start.2 = (bf16[2,128,896]{2,1,0:T(8,128)(2,1)S(1)}, bf16[2,128,896]{2,1,0:T(8,128)(2,1)S(1)}, u32[]{:S(2)}, u32[]{:S(2)}) collective-permute-start(bf16[2,128,896]{2,1,0:T(8,128)(2,1)S(1)} %get-tuple-element.31.own_ref), channel_id=1, source_target_pairs={{0,1},{1,0},{2,3},{3,2},{4,5},{5,4},{6,7},{7,6},{8,9},{9,8},{10,11... | collective-permute-start | bytes 1376264 | tf_op jit(solution)/shard_map/ppermute | solution.py:319
  41.0 16.9 %collective-permute-start.5 = (bf16[512,512]{1,0:T(8,128)(2,1)S(1)}, bf16[512,512]{1,0:T(8,128)(2,1)S(1)}, u32[]{:S(2)}, u32[]{:S(2)}) collective-permute-start(bf16[512,512]{1,0:T(8,128)(2,1)S(1)} %all_gather.3.refs_0_), channel_id=1, source_target_pairs={{0,448},{1,449},{2,450},{3,451},{4,452},{5,453},{6,454},{7,455},{8... | collective-permute-start | bytes 1572872 | tf_op jit(solution)/shard_map/ppermute | solution.py:59
  44.3 15.7 %collective-permute-start.3 = (bf16[512,512]{1,0:T(8,128)(2,1)S(1)}, bf16[512,512]{1,0:T(8,128)(2,1)S(1)}, u32[]{:S(2)}, u32[]{:S(2)}) collective-permute-start(bf16[512,512]{1,0:T(8,128)(2,1)S(1)} %all_gather.3.refs_0_), channel_id=1, source_target_pairs={{0,64},{1,65},{2,66},{3,67},{4,68},{5,69},{6,70},{7,71},{8,72},{9,... | collective-permute-start | bytes 1572872 | tf_op jit(solution)/shard_map/ppermute | solution.py:59
  58.0 16.2 %collective-permute-start.7 = (bf16[512,512]{1,0:T(8,128)(2,1)S(1)}, bf16[512,512]{1,0:T(8,128)(2,1)S(1)}, u32[]{:S(2)}, u32[]{:S(2)}) collective-permute-start(bf16[512,512]{1,0:T(8,128)(2,1)S(1)} %collective-permute-done.5.refs_1_), channel_id=1, source_target_pairs={{0,448},{1,449},{2,450},{3,451},{4,452},{5,453},{6,454},{7,455},{8... | collective-permute-start | bytes 1572872 | tf_op jit(solution)/shard_map/ppermute | solution.py:59
  60.0 16.1 %collective-permute-start.4 = (bf16[512,512]{1,0:T(8,128)(2,1)S(1)}, bf16[512,512]{1,0:T(8,128)(2,1)S(1)}, u32[]{:S(2)}, u32[]{:S(2)}) collective-permute-start(bf16[512,512]{1,0:T(8,128)(2,1)S(1)} %collective-permute-done.3.refs_0_), channel_id=1, source_target_pairs={{0,64},{1,65},{2,66},{3,67},{4,68},{5,69},{6,70},{7,71},{8,72},{9,... | collective-permute-start | bytes 1572872 | tf_op jit(solution)/shard_map/ppermute | solution.py:59
  74.2 16.1 %collective-permute-start.9 = (bf16[512,512]{1,0:T(8,128)(2,1)S(1)}, bf16[512,512]{1,0:T(8,128)(2,1)S(1)}, u32[]{:S(2)}, u32[]{:S(2)}) collective-permute-start(bf16[512,512]{1,0:T(8,128)(2,1)S(1)} %collective-permute-done.7.refs_1_), channel_id=1, source_target_pairs={{0,448},{1,449},{2,450},{3,451},{4,452},{5,453},{6,454},{7,455},{8... | collective-permute-start | bytes 1572872 | tf_op jit(solution)/shard_map/ppermute | solution.py:59
  76.2 16.1 %collective-permute-start.6 = (bf16[512,512]{1,0:T(8,128)(2,1)S(1)}, bf16[512,512]{1,0:T(8,128)(2,1)S(1)}, u32[]{:S(2)}, u32[]{:S(2)}) collective-permute-start(bf16[512,512]{1,0:T(8,128)(2,1)S(1)} %collective-permute-done.4.refs_0_), channel_id=1, source_target_pairs={{0,64},{1,65},{2,66},{3,67},{4,68},{5,69},{6,70},{7,71},{8,72},{9,... | collective-permute-start | bytes 1572872 | tf_op jit(solution)/shard_map/ppermute | solution.py:59
  90.3 16.3 %collective-permute-start.10 = (bf16[256,512]{1,0:T(8,128)(2,1)S(1)}, bf16[256,512]{1,0:T(8,128)(2,1)S(1)}, u32[]{:S(2)}, u32[]{:S(2)}) collective-permute-start(bf16[256,512]{1,0:T(8,128)(2,1)S(1)} %slice.37), channel_id=1, source_target_pairs={{0,448},{1,449},{2,450},{3,451},{4,452},{5,453},{6,454},{7,455},{8... | collective-permute-start | bytes 786440 | tf_op jit(solution)/shard_map/ppermute | solution.py:59
  92.3 14.4 %collective-permute-start.8 = (bf16[256,512]{1,0:T(8,128)(2,1)S(1)}, bf16[256,512]{1,0:T(8,128)(2,1)S(1)}, u32[]{:S(2)}, u32[]{:S(2)}) collective-permute-start(bf16[256,512]{1,0:T(8,128)(2,1)S(1)} %slice.36), channel_id=1, source_target_pairs={{0,64},{1,65},{2,66},{3,67},{4,68},{5,69},{6,70},{7,71},{8,72},{9,... | collective-permute-start | bytes 786440 | tf_op jit(solution)/shard_map/ppermute | solution.py:59
  113.0 5.7 %collective-permute-start.11 = (f32[2,896,256]{2,1,0:T(8,128)S(1)}, f32[2,896,256]{2,1,0:T(8,128)S(1)}, u32[]{:S(2)}, u32[]{:S(2)}) collective-permute-start(f32[2,896,256]{2,1,0:T(8,128)S(1)} %get-tuple-element.52), channel_id=1, source_target_pairs={{0,1},{1,0},{2,3},{3,2},{4,5},{5,4},{6,7},{7,6},{8,9},{9,8},{10,11... | collective-permute-start | bytes 5505032 | tf_op jit(solution)/shard_map/ppermute | solution.py:341
  120.0 13.8 %collective-permute-start.12 = (bf16[128,896]{1,0:T(8,128)(2,1)S(1)}, bf16[128,896]{1,0:T(8,128)(2,1)S(1)}, u32[]{:S(2)}, u32[]{:S(2)}) collective-permute-start(bf16[128,896]{1,0:T(8,128)(2,1)S(1)} %get-tuple-element.57), channel_id=1, source_target_pairs={{2,0},{3,4},{7,8},{6,12},{10,1},{11,5},{15,9},{14,13},{0,2},{1,6},... | collective-permute-start | bytes 688136 | tf_op jit(solution)/shard_map/ppermute | solution.py:350
  127.5 13.5 %collective-permute-start.13 = (bf16[128,896]{1,0:T(8,128)(2,1)S(1)}, bf16[128,896]{1,0:T(8,128)(2,1)S(1)}, u32[]{:S(2)}, u32[]{:S(2)}) collective-permute-start(bf16[128,896]{1,0:T(8,128)(2,1)S(1)} %get-tuple-element.58), channel_id=1, source_target_pairs={{6,0},{7,4},{3,8},{2,12},{14,1},{15,5},{11,9},{10,13},{4,2},{5,6},... | collective-permute-start | bytes 688136 | tf_op jit(solution)/shard_map/ppermute | solution.py:351
where the time goes:
time: 142 us
  starting transfers between devices  53.2 us (37%)
  Pallas kernels  41.7 us (29%)
  waiting for transfers between devices  28.9 us (20%)
  blocking collectives  13.6 us (10%)
  local copies, waits for them, and re-layouts  1.99 us (1%)
  other arithmetic  1.91 us (1%)
    pallas_call x5, Pallas kernels, attend(): pl.pallas_call(functools.partial(attend_kernel, first, last, offsets), ou...  38.7 us
    ppermute x8, starting transfers between devices, shifted(): return lax.ppermute(array, ('seq', 'stretch'), plane_shift(dx, dy))  28.4 us
    all_gather x1, blocking collectives, on_device(): lax.all_gather(own, 'seq', axis=0, tiled=True, axis_index_groups=lines)  13.6 us
    ppermute x1, waiting for transfers between devices, on_device(): two = lax.ppermute(jnp.where(low, packs[1], packs[0]), 'stretch', crossed)  10.2 us
    ppermute x1, starting transfers between devices, on_device(): one = lax.ppermute(merged[0], 'stretch', back(straight))  7.48 us
    ppermute x1, waiting for transfers between devices, on_device(): two = lax.ppermute(merged[1], 'stretch', back(crossed))  7.1 us
    ppermute x1, starting transfers between devices, on_device(): two = lax.ppermute(jnp.where(low, packs[1], packs[0]), 'stretch', crossed)  5.54 us
    ppermute x1, waiting for transfers between devices, on_device(): one = lax.ppermute(merged[0], 'stretch', back(straight))  4.43 us
  transfers between devices with their start and end apart: 14, of which 5 were waited for; matrix products, arithmetic and copies ran while one was open for 1% of the time, Pallas kernels for 24%

commit v1 on v0

--- a/solution.py
+++ b/solution.py
@@ -75,20 +75,19 @@
 SMEM = pl.BlockSpec(memory_space=pltpu.SMEM)
 
 
-def unpack_kernel(where_ref, one_ref, two_ref, cosine_ref, sine_ref, out_ref, raw_ref):
+def key_kernel(where_ref, one_ref, two_ref, cosine_ref, sine_ref, out_ref):
     head = where_ref[0]
     cosine = cosine_ref[0]
     sine = sine_ref[0]
     for k, ref in enumerate((one_ref, two_ref)):
-        slot = head ^ k
-        place = pl.multiple_of(slot * (2 * HEAD_SIZE), 2 * HEAD_SIZE)
+        place = pl.multiple_of((head ^ k) * (2 * HEAD_SIZE), 2 * HEAD_SIZE)
         x = ref[:, :HEAD_SIZE].astype(jnp.float32)
         out_ref[:, pl.ds(place, HEAD_SIZE)] = spin(x, cosine, sine).astype(jnp.bfloat16)
         out_ref[:, pl.ds(place + HEAD_SIZE, HEAD_SIZE)] = ref[:, HEAD_SIZE : 2 * HEAD_SIZE]
-        raw_ref[slot] = ref[:, 2 * HEAD_SIZE :]
 
 
 def query_kernel(where_ref, own_ref, other_ref, cosine_ref, sine_ref, out_ref):
+    head = where_ref[0]
     core = where_ref[1]
 
     def turn(ref, which, kind, slot):
@@ -98,19 +97,19 @@
             x = ref[which, :, g * HEAD_SIZE : (g + 1) * HEAD_SIZE].astype(jnp.float32)
             out_ref[slot, g * ROWS : (g + 1) * ROWS, :] = spin(x, cosine, sine).astype(jnp.bfloat16)
 
-    turn(own_ref, 0, 0, 0)
-    turn(own_ref, 1, 0, 1)
-    turn(other_ref, 1, 2, 3)
+    turn(own_ref, head, 0, 0)
+    turn(own_ref, 1 - head, 0, 1)
+    turn(other_ref, 1 - head, 2, 3)
 
     @pl.when(core == 0)
     def _():
-        turn(other_ref, 0, 1, 2)
-        turn(own_ref, 1, 2, 4)
+        turn(other_ref, head, 1, 2)
+        turn(own_ref, 1 - head, 2, 4)
 
     @pl.when(core == 1)
     def _():
-        turn(own_ref, 1, 1, 2)
-        turn(other_ref, 1, 1, 4)
+        turn(own_ref, 1 - head, 1, 2)
+        turn(other_ref, 1 - head, 1, 4)
 
 
 def lanes(x, count):
@@ -165,7 +164,7 @@
 
 
 def attend_kernel(first, last, offsets, where_ref, query_ref, *refs):
-    number = len(offsets)
+    number = 1 if first else len(offsets)
     block_refs = refs[:number]
     refs = refs[number:]
     if last:
@@ -192,10 +191,10 @@
         values = ref[:, pl.ds(place + HEAD_SIZE, HEAD_SIZE)]
         return keys, values
 
-    def causal(ref, limit):
+    def causal(refs, limit):
         def body(query, carry):
             place = pl.multiple_of(query * (2 * HEAD_SIZE), 2 * HEAD_SIZE)
-            run(query=query, pairs=[columns(ref, place)], slot=query, limit=limit)
+            run(query=query, pairs=[columns(ref, place) for ref in refs], slot=query, limit=limit)
             return carry
 
         lax.fori_loop(0, 2, body, 0)
@@ -208,13 +207,13 @@
     run(query=4, pairs=pairs, slot=1 + 2 * core, limit=None)
     if first:
         column = lax.broadcasted_iota(jnp.int32, (CHUNK, SPAN), 1)
-        causal(block_refs[0], (column, x * ROWS))
+        causal(block_refs[:1], (column, x * ROWS))
     else:
-        for b in range(number):
-
-            @pl.when(((y + offsets[b]) & (Y - 1)) < y)
-            def _(b=b):
-                causal(block_refs[b], None)
+        for offset in sorted(set(offsets)):
+
+            @pl.when(((y + offset) & (Y - 1)) < y)
+            def _(offset=offset):
+                causal([block_refs[b] for b in range(number) if offsets[b] == offset], None)
 
     if last:
         lane = lax.broadcasted_iota(jnp.int32, (STACKED, HEAD_SIZE), 1)
@@ -289,33 +288,33 @@
     straight, crossed = stretch_pairs(0), stretch_pairs(1)
 
     half = GROUP * HEAD_SIZE
+
+    def halves_of(first, second):
+        return jnp.where(low, first, second), jnp.where(low, second, first)
+
+    def spread(first, second):
+        one = lax.ppermute(first, "stretch", straight)
+        two = lax.ppermute(second, "stretch", crossed)
+        return one, two
+
     packs = [
-        jnp.concatenate(
-            [
-                keys[:, k * HEAD_SIZE : (k + 1) * HEAD_SIZE],
-                values[:, k * HEAD_SIZE : (k + 1) * HEAD_SIZE],
-                queries[:, k * half : (k + 1) * half],
-            ],
-            axis=1,
-        )
-        for k in range(KEY_VALUE_HEADS)
+        jnp.concatenate([keys[:, k : k + HEAD_SIZE], values[:, k : k + HEAD_SIZE]], axis=1)
+        for k in (0, HEAD_SIZE)
     ]
-    one = lax.ppermute(jnp.where(low, packs[0], packs[1]), "stretch", straight)
-    two = lax.ppermute(jnp.where(low, packs[1], packs[0]), "stretch", crossed)
-    own, raw = pl.pallas_call(
-        unpack_kernel,
-        out_shape=[
-            jax.ShapeDtypeStruct((ROWS, 4 * HEAD_SIZE), jnp.bfloat16),
-            jax.ShapeDtypeStruct((2, ROWS, half), jnp.bfloat16),
-        ],
+    one, two = spread(*halves_of(*packs))
+    own = pl.pallas_call(
+        key_kernel,
+        out_shape=jax.ShapeDtypeStruct((ROWS, 4 * HEAD_SIZE), jnp.bfloat16),
         in_specs=[SMEM] + [VMEM] * 4,
-        out_specs=[VMEM] * 2,
+        out_specs=VMEM,
         compiler_params=pltpu.CompilerParams(vmem_limit_bytes=8 << 20),
-        name="unpack",
+        name="turn_keys",
     )(base, one, two, cosine, sine)
     lines = [[X * line + k for k in range(X)] for line in range(Y)]
     row = lax.all_gather(own, "seq", axis=0, tiled=True, axis_index_groups=lines)
-    row, raw = lax.optimization_barrier((row, raw))
+    straight_half, crossed_half = halves_of(queries[:, :half], queries[:, half:])
+    row, crossed_half = lax.optimization_barrier((row, crossed_half))
+    raw = jnp.stack(spread(straight_half, crossed_half))
     other_raw = lax.ppermute(raw, "stretch", SWAP)
     query = pl.pallas_call(
         query_kernel,
@@ -326,18 +325,29 @@
         compiler_params=pltpu.CompilerParams(vmem_limit_bytes=12 << 20),
         name="turn_queries",
     )(base, raw, other_raw, cosine, sine)
-    up, down = row, row
-    blocks, offsets, state = [row], (0,), []
-    for hop in range(1, Y // 2 + 1):
+    rounds = [(row,)]
+    states = []
+
+    def step(hop, ahead):
+        up, down = rounds[-1][0], rounds[-1][-1]
         if hop == Y // 2:
             up, down = up[: SPAN // 2], down[SPAN // 2 :]
-        next_up = shifted(up, 0, 1)
-        next_down = shifted(down, 0, -1)
-        state = attend(base, query, blocks, offsets, state, first=hop == 1)
-        up, _ = lax.optimization_barrier((next_up, state[2]))
-        down, _ = lax.optimization_barrier((next_down, state[2]))
-        blocks, offsets = [next_up, next_down], (-hop, hop)
-    mine, send = attend(base, query, blocks, (4, 4), state, last=True)
+        if ahead is not None:
+            up, _ = lax.optimization_barrier((up, ahead))
+            down, _ = lax.optimization_barrier((down, ahead))
+        rounds.append((shifted(up, 0, 1), shifted(down, 0, -1)))
+
+    step(1, None)
+    step(2, None)
+    for hop in range(Y // 2):
+        states.append(
+            attend(
+                base, query, rounds[hop], (-hop, hop), states[-1] if states else [], first=hop == 0
+            )
+        )
+        if hop < 2:
+            step(hop + 3, states[-1][2])
+    mine, send = attend(base, query, rounds[4], (4, 4), states[-1], last=True)
     received = lax.ppermute(send, "stretch", SWAP)
     merged = pl.pallas_call(
         merge_kernel,

time: 142 us -> 140 us (0.986); the launches traced: 142 us -> 138 us
  waiting for transfers between devices: 28.9 us -> 21.8 us
  starting transfers between devices: 53.2 us -> 56.7 us
    ppermute x2 -> x4, waiting for transfers between devices: 10.2 us -> 1.6 us  [the longest x2 1.59 us: spread(): two = lax.ppermute(second, 'stretch', crossed)]
    ppermute x2 -> x4, starting transfers between devices: 9.82 us -> 18.1 us  [the longest x2 11.9 us: spread(): two = lax.ppermute(second, 'stretch', crossed)]
    ppermute x1, starting transfers between devices: 7.48 us -> 2.26 us  [on_device(): one = lax.ppermute(merged[0], 'stretch', back(straight))]
    ppermute x8, waiting for transfers between devices: 3.46 us -> 8.45 us  [shifted(): return lax.ppermute(array, ('seq', 'stretch'), plane_shift(dx, dy))]
    ppermute x8, starting transfers between devices: 28.4 us -> 25.3 us  [shifted(): return lax.ppermute(array, ('seq', 'stretch'), plane_shift(dx, dy))]
    ppermute x1, waiting for transfers between devices: 7.1 us -> 4.62 us  [on_device(): two = lax.ppermute(merged[1], 'stretch', back(crossed))]
    ppermute x1, starting transfers between devices: 1.92 us -> 4.24 us  [on_device(): two = lax.ppermute(merged[1], 'stretch', back(crossed))]
  transfers between devices with their start and end apart: 14 -> 16, of which waited for: 5 -> 7; matrix products, arithmetic and copies ran while one was open for 1% -> 2% of each run, Pallas kernels for 24% -> 25%
where the time goes in v1:
time: 140 us; the launch traced here: 138 us
  starting transfers between devices  56.7 us (40%)
  Pallas kernels  41.2 us (29%)
  waiting for transfers between devices  21.8 us (16%)
  blocking collectives  13.8 us (10%)
  other arithmetic  2.98 us (2%)
    pallas_call x5, Pallas kernels, attend(): pl.pallas_call(functools.partial(attend_kernel, first, last, offsets), ou...  38.2 us
    ppermute x8, starting transfers between devices, shifted(): return lax.ppermute(array, ('seq', 'stretch'), plane_shift(dx, dy))  25.3 us
    all_gather x1, blocking collectives, on_device(): lax.all_gather(own, 'seq', axis=0, tiled=True, axis_index_groups=lines)  13.8 us
    ppermute x2, starting transfers between devices, spread(): two = lax.ppermute(second, 'stretch', crossed)  11.9 us
    ppermute x8, waiting for transfers between devices, shifted(): return lax.ppermute(array, ('seq', 'stretch'), plane_shift(dx, dy))  8.45 us
    ppermute x2, starting transfers between devices, spread(): one = lax.ppermute(first, 'stretch', straight)  6.2 us
    ppermute x1, starting transfers between devices, on_device(): other_raw = lax.ppermute(raw, 'stretch', SWAP)  4.87 us
    ppermute x1, waiting for transfers between devices, on_device(): two = lax.ppermute(merged[1], 'stretch', back(crossed))  4.62 us
  transfers between devices with their start and end apart: 16, of which 7 were waited for; matrix products, arithmetic and copies ran while one was open for 2% of the time, Pallas kernels for 25%

profile of v1, /device:TPU:56, one launch (start us, length us, event | category | flops | bytes accessed | tf_op | source)
XLA Modules:
  0.0 137.8 jit_solution(5636249734579542775)
XLA Ops:
  0.0 0.8 fusion.5
  0.9 4.3 %collective-permute-start.1 = (bf16[128,256]{1,0:T(8,128)(2,1)S(1)}, bf16[128,256]{1,0:T(8,128)(2,1)S(1)}, u32[]{:S(2)}, u32[]{:S(2)}) collective-permute-start(bf16[128,256]{1,0:T(8,128)(2,1)S(1)} %get-tuple-element.52), channel_id=1, source_target_pairs={{0,2},{4,3},{8,7},{12,6},{1,10},{5,11},{9,15},{13,14},{2,0},{6,1},... | collective-permute-start | bytes 196616 | tf_op jit(solution)/shard_map/ppermute | solution.py:296
  5.1 5.5 %collective-permute-start.2 = (bf16[128,256]{1,0:T(8,128)(2,1)S(1)}, bf16[128,256]{1,0:T(8,128)(2,1)S(1)}, u32[]{:S(2)}, u32[]{:S(2)}) collective-permute-start(bf16[128,256]{1,0:T(8,128)(2,1)S(1)} %get-tuple-element.51), channel_id=1, source_target_pairs={{0,6},{4,7},{8,3},{12,2},{1,14},{5,15},{9,11},{13,10},{2,4},{6,5},... | collective-permute-start | bytes 196616 | tf_op jit(solution)/shard_map/ppermute | solution.py:297
  10.7 1.1 broadcast_select_fusion.3
  11.8 1.9 %collective-permute-start = (bf16[128,896]{1,0:T(8,128)(2,1)S(1)}, bf16[128,896]{1,0:T(8,128)(2,1)S(1)}, u32[]{:S(2)}, u32[]{:S(2)}) collective-permute-start(bf16[128,896]{1,0:T(8,128)(2,1)S(1)} %get-tuple-element.49), channel_id=1, source_target_pairs={{0,2},{4,3},{8,7},{12,6},{1,10},{5,11},{9,15},{13,14},{2,0},{6,1},... | collective-permute-start | bytes 688136 | tf_op jit(solution)/shard_map/ppermute | solution.py:296
  14.8 1.4 %collective-permute-done.2.two_ref = bf16[128,256]{1,0:T(8,128)(2,1)S(1)} collective-permute-done((bf16[128,256]{1,0:T(8,128)(2,1)S(1)}, bf16[128,256]{1,0:T(8,128)(2,1)S(1)}, u32[]{:S(2)}, u32[]{:S(2)}) %collective-permute-start.2) | collective-permute-done | bytes 65568 | tf_op jit(solution)/shard_map/ppermute | solution.py:297
  16.9 13.8 %all_gather.3.refs_0_ = bf16[512,512]{1,0:T(8,128)(2,1)S(1)} all-gather(bf16[128,512]{1,0:T(8,128)(2,1)S(1)} %turn_keys.1), channel_id=1, replica_groups={{0,16,32,48},{64,80,96,112},{128,144,160,176},{192,208,224,240},{256,27..., dimensions={0}, use_global_device_ids=true | all-gather | bytes 655360 | tf_op jit(solution)/shard_map/all_gather | solution.py:314
  30.7 6.4 %collective-permute-start.3 = (bf16[128,896]{1,0:T(8,128)(2,1)S(1)}, bf16[128,896]{1,0:T(8,128)(2,1)S(1)}, u32[]{:S(2)}, u32[]{:S(2)}) collective-permute-start(bf16[128,896]{1,0:T(8,128)(2,1)S(1)} %get-tuple-element.25), channel_id=1, source_target_pairs={{0,6},{4,7},{8,3},{12,2},{1,14},{5,15},{9,11},{13,10},{2,4},{6,5},... | collective-permute-start | bytes 688136 | tf_op jit(solution)/shard_map/ppermute | solution.py:297
  37.1 1.9 %collective-permute-start.5 = (bf16[512,512]{1,0:T(8,128)(2,1)S(1)}, bf16[512,512]{1,0:T(8,128)(2,1)S(1)}, u32[]{:S(2)}, u32[]{:S(2)}) collective-permute-start(bf16[512,512]{1,0:T(8,128)(2,1)S(1)} %all_gather.3.refs_0_), channel_id=1, source_target_pairs={{0,64},{1,65},{2,66},{3,67},{4,68},{5,69},{6,70},{7,71},{8,72},{9,... | collective-permute-start | bytes 1572872 | tf_op jit(solution)/shard_map/ppermute | solution.py:59
  39.0 3.9 %collective-permute-start.8 = (bf16[512,512]{1,0:T(8,128)(2,1)S(1)}, bf16[512,512]{1,0:T(8,128)(2,1)S(1)}, u32[]{:S(2)}, u32[]{:S(2)}) collective-permute-start(bf16[512,512]{1,0:T(8,128)(2,1)S(1)} %all_gather.3.refs_0_), channel_id=1, source_target_pairs={{0,448},{1,449},{2,450},{3,451},{4,452},{5,453},{6,454},{7,455},{8... | collective-permute-start | bytes 1572872 | tf_op jit(solution)/shard_map/ppermute | solution.py:59
  43.1 4.9 %collective-permute-start.4 = (bf16[2,128,896]{2,1,0:T(8,128)(2,1)S(1)}, bf16[2,128,896]{2,1,0:T(8,128)(2,1)S(1)}, u32[]{:S(2)}, u32[]{:S(2)}) collective-permute-start(bf16[2,128,896]{2,1,0:T(8,128)(2,1)S(1)} %pad_maximum_fusion.own_ref), channel_id=1, source_target_pairs={{0,1},{1,0},{2,3},{3,2},{4,5},{5,4},{6,7},{7,6},{8,9},{9,8},{10,11... | collective-permute-start | bytes 1376264 | tf_op jit(solution)/shard_map/ppermute | solution.py:318
  48.0 5.3 %collective-permute-done.5.refs_0_ = bf16[512,512]{1,0:T(8,128)(2,1)S(1)} collective-permute-done((bf16[512,512]{1,0:T(8,128)(2,1)S(1)}, bf16[512,512]{1,0:T(8,128)(2,1)S(1)}, u32[]{:S(2)}, u32[]{:S(2)}) %collective-permute-start.5) | collective-permute-done | bytes 524320 | tf_op jit(solution)/shard_map/ppermute | solution.py:59
  53.3 3.4 %collective-permute-start.6 = (bf16[512,512]{1,0:T(8,128)(2,1)S(1)}, bf16[512,512]{1,0:T(8,128)(2,1)S(1)}, u32[]{:S(2)}, u32[]{:S(2)}) collective-permute-start(bf16[512,512]{1,0:T(8,128)(2,1)S(1)} %collective-permute-done.5.refs_0_), channel_id=1, source_target_pairs={{0,64},{1,65},{2,66},{3,67},{4,68},{5,69},{6,70},{7,71},{8,72},{9,... | collective-permute-start | bytes 1572872 | tf_op jit(solution)/shard_map/ppermute | solution.py:59
  56.8 2.4 %collective-permute-start.10 = (bf16[512,512]{1,0:T(8,128)(2,1)S(1)}, bf16[512,512]{1,0:T(8,128)(2,1)S(1)}, u32[]{:S(2)}, u32[]{:S(2)}) collective-permute-start(bf16[512,512]{1,0:T(8,128)(2,1)S(1)} %collective-permute-done.8.refs_1_), channel_id=1, source_target_pairs={{0,448},{1,449},{2,450},{3,451},{4,452},{5,453},{6,454},{7,455},{8... | collective-permute-start | bytes 1572872 | tf_op jit(solution)/shard_map/ppermute | solution.py:59
  59.2 1.1 turn_queries.1.query_ref
  60.3 5.3 %attend.5 = (f32[4,896,128]{2,1,0:T(8,128)S(1)}, f32[4,896,128]{2,1,0:T(8,128)S(1)}, f32[4,896,128]{2,1,0:T(8,128)S(1)}) custom-call(s32[4]{0:T(128)S(1)} %pad_add_fusion.where_ref, bf16[5,896,128]{2,1,0:T(8,128)(2,1)S(1)} %turn_queries.1.query_ref, bf16[512,512]{1,0:T(8,128)(2,1)S(1)} %all_gather.3.refs_0_), custom_call_target="tpu_custom_call" | custom-call | flops 939524096 | bytes 4194304 | tf_op jit(solution)/shard_map/attend/pallas_call | solution.py:234
  65.7 3.1 %collective-permute-done.6.refs_0_ = bf16[512,512]{1,0:T(8,128)(2,1)S(1)} collective-permute-done((bf16[512,512]{1,0:T(8,128)(2,1)S(1)}, bf16[512,512]{1,0:T(8,128)(2,1)S(1)}, u32[]{:S(2)}, u32[]{:S(2)}) %collective-permute-start.6) | collective-permute-done | bytes 524320 | tf_op jit(solution)/shard_map/ppermute | solution.py:59
  68.8 4.9 %collective-permute-start.7 = (bf16[512,512]{1,0:T(8,128)(2,1)S(1)}, bf16[512,512]{1,0:T(8,128)(2,1)S(1)}, u32[]{:S(2)}, u32[]{:S(2)}) collective-permute-start(bf16[512,512]{1,0:T(8,128)(2,1)S(1)} %collective-permute-done.6.refs_0_), channel_id=1, source_target_pairs={{0,64},{1,65},{2,66},{3,67},{4,68},{5,69},{6,70},{7,71},{8,72},{9,... | collective-permute-start | bytes 1572872 | tf_op jit(solution)/shard_map/ppermute | solution.py:59
  73.7 1.9 %collective-permute-start.11 = (bf16[512,512]{1,0:T(8,128)(2,1)S(1)}, bf16[512,512]{1,0:T(8,128)(2,1)S(1)}, u32[]{:S(2)}, u32[]{:S(2)}) collective-permute-start(bf16[512,512]{1,0:T(8,128)(2,1)S(1)} %collective-permute-done.10.refs_1_), channel_id=1, source_target_pairs={{0,448},{1,449},{2,450},{3,451},{4,452},{5,453},{6,454},{7,455},{8... | collective-permute-start | bytes 1572872 | tf_op jit(solution)/shard_map/ppermute | solution.py:59
  75.6 9.2 %attend.6 = (f32[4,896,128]{2,1,0:T(8,128)S(1)}, f32[4,896,128]{2,1,0:T(8,128)S(1)}, f32[4,896,128]{2,1,0:T(8,128)S(1)}) custom-call(s32[4]{0:T(128)S(1)} %pad_add_fusion.where_ref, bf16[5,896,128]{2,1,0:T(8,128)(2,1)S(1)} %turn_queries.1.query_ref, bf16[512,512]{1,0:T(8,128)(2,1)S(1)} %collective-permute-done.5.refs_0_, ...), custom_call_target="tpu_custom_call" | custom-call | flops 1879048192 | bytes 4194304 | tf_op jit(solution)/shard_map/attend/pallas_call | solution.py:234
  84.8 4.9 %collective-permute-start.9 = (bf16[256,512]{1,0:T(8,128)(2,1)S(1)}, bf16[256,512]{1,0:T(8,128)(2,1)S(1)}, u32[]{:S(2)}, u32[]{:S(2)}) collective-permute-start(bf16[256,512]{1,0:T(8,128)(2,1)S(1)} %slice.40), channel_id=1, source_target_pairs={{0,64},{1,65},{2,66},{3,67},{4,68},{5,69},{6,70},{7,71},{8,72},{9,... | collective-permute-start | bytes 786440 | tf_op jit(solution)/shard_map/ppermute | solution.py:59
  89.8 1.9 %collective-permute-start.12 = (bf16[256,512]{1,0:T(8,128)(2,1)S(1)}, bf16[256,512]{1,0:T(8,128)(2,1)S(1)}, u32[]{:S(2)}, u32[]{:S(2)}) collective-permute-start(bf16[256,512]{1,0:T(8,128)(2,1)S(1)} %slice.41), channel_id=1, source_target_pairs={{0,448},{1,449},{2,450},{3,451},{4,452},{5,453},{6,454},{7,455},{8... | collective-permute-start | bytes 786440 | tf_op jit(solution)/shard_map/ppermute | solution.py:59
  91.7 9.2 %attend.7 = (f32[4,896,128]{2,1,0:T(8,128)S(1)}, f32[4,896,128]{2,1,0:T(8,128)S(1)}, f32[4,896,128]{2,1,0:T(8,128)S(1)}) custom-call(s32[4]{0:T(128)S(1)} %pad_add_fusion.where_ref, bf16[5,896,128]{2,1,0:T(8,128)(2,1)S(1)} %turn_queries.1.query_ref, bf16[512,512]{1,0:T(8,128)(2,1)S(1)} %collective-permute-done.6.refs_0_, ...), custom_call_target="tpu_custom_call" | custom-call | flops 1879048192 | bytes 4194304 | tf_op jit(solution)/shard_map/attend/pallas_call | solution.py:234
  100.9 9.0 %attend.8 = (f32[4,896,128]{2,1,0:T(8,128)S(1)}, f32[4,896,128]{2,1,0:T(8,128)S(1)}, f32[4,896,128]{2,1,0:T(8,128)S(1)}) custom-call(s32[4]{0:T(128)S(1)} %pad_add_fusion.where_ref, bf16[5,896,128]{2,1,0:T(8,128)(2,1)S(1)} %turn_queries.1.query_ref, bf16[512,512]{1,0:T(8,128)(2,1)S(1)} %collective-permute-done.7.refs_0_, ...), custom_call_target="tpu_custom_call" | custom-call | flops 1879048192 | bytes 4194304 | tf_op jit(solution)/shard_map/attend/pallas_call | solution.py:234
  109.9 5.5 %attend.9 = (f32[2,896,256]{2,1,0:T(8,128)S(1)}, f32[2,896,256]{2,1,0:T(8,128)S(1)}) custom-call(s32[4]{0:T(128)S(1)} %pad_add_fusion.where_ref, bf16[5,896,128]{2,1,0:T(8,128)(2,1)S(1)} %turn_queries.1.query_ref, bf16[256,512]{1,0:T(8,128)(2,1)S(1)} %collective-permute-done.9.refs_0_, bf16[256,512]{1,0:T(8,128)(2,1)S(1)} %collective-permute-done.12.refs_1_, ...), custom_call_target="tpu_custom_call" | custom-call | flops 1879048192 | bytes 4194304 | tf_op jit(solution)/shard_map/attend/pallas_call | solution.py:234
  115.4 1.9 %collective-permute-start.13 = (f32[2,896,256]{2,1,0:T(8,128)S(1)}, f32[2,896,256]{2,1,0:T(8,128)S(1)}, u32[]{:S(2)}, u32[]{:S(2)}) collective-permute-start(f32[2,896,256]{2,1,0:T(8,128)S(1)} %get-tuple-element.44), channel_id=1, source_target_pairs={{0,1},{1,0},{2,3},{3,2},{4,5},{5,4},{6,7},{7,6},{8,9},{9,8},{10,11... | collective-permute-start | bytes 5505032 | tf_op jit(solution)/shard_map/ppermute | solution.py:351
  117.4 3.8 %collective-permute-done.13.other_ref = f32[2,896,256]{2,1,0:T(8,128)S(1)} collective-permute-done((f32[2,896,256]{2,1,0:T(8,128)S(1)}, f32[2,896,256]{2,1,0:T(8,128)S(1)}, u32[]{:S(2)}, u32[]{:S(2)}) %collective-permute-start.13) | collective-permute-done | bytes 1835040 | tf_op jit(solution)/shard_map/ppermute | solution.py:351
  121.1 1.3 merge.1
  122.4 2.3 %collective-permute-start.14 = (bf16[128,896]{1,0:T(8,128)(2,1)S(1)}, bf16[128,896]{1,0:T(8,128)(2,1)S(1)}, u32[]{:S(2)}, u32[]{:S(2)}) collective-permute-start(bf16[128,896]{1,0:T(8,128)(2,1)S(1)} %get-tuple-element.47), channel_id=1, source_target_pairs={{2,0},{3,4},{7,8},{6,12},{10,1},{11,5},{15,9},{14,13},{0,2},{1,6},... | collective-permute-start | bytes 688136 | tf_op jit(solution)/shard_map/ppermute | solution.py:360
  124.7 4.2 %collective-permute-start.15 = (bf16[128,896]{1,0:T(8,128)(2,1)S(1)}, bf16[128,896]{1,0:T(8,128)(2,1)S(1)}, u32[]{:S(2)}, u32[]{:S(2)}) collective-permute-start(bf16[128,896]{1,0:T(8,128)(2,1)S(1)} %get-tuple-element.48), channel_id=1, source_target_pairs={{6,0},{7,4},{3,8},{2,12},{14,1},{15,5},{11,9},{10,13},{4,2},{5,6},... | collective-permute-start | bytes 688136 | tf_op jit(solution)/shard_map/ppermute | solution.py:361
  129.0 3.4 %collective-permute-done.14 = bf16[128,896]{1,0:T(8,128)(2,1)S(1)} collective-permute-done((bf16[128,896]{1,0:T(8,128)(2,1)S(1)}, bf16[128,896]{1,0:T(8,128)(2,1)S(1)}, u32[]{:S(2)}, u32[]{:S(2)}) %collective-permute-start.14) | collective-permute-done | bytes 229408 | tf_op jit(solution)/shard_map/ppermute | solution.py:360
  132.3 4.6 %collective-permute-done.15 = bf16[128,896]{1,0:T(8,128)(2,1)S(1)} collective-permute-done((bf16[128,896]{1,0:T(8,128)(2,1)S(1)}, bf16[128,896]{1,0:T(8,128)(2,1)S(1)}, u32[]{:S(2)}, u32[]{:S(2)}) %collective-permute-start.15) | collective-permute-done | bytes 229408 | tf_op jit(solution)/shard_map/ppermute | solution.py:361
  (26 shorter events, 2.8 us)
Async XLA Ops:
  0.9 13.9 %collective-permute-start.1 = (bf16[128,256]{1,0:T(8,128)(2,1)S(1)}, bf16[128,256]{1,0:T(8,128)(2,1)S(1)}, u32[]{:S(2)}, u32[]{:S(2)}) collective-permute-start(bf16[128,256]{1,0:T(8,128)(2,1)S(1)} %get-tuple-element.52), channel_id=1, source_target_pairs={{0,2},{4,3},{8,7},{12,6},{1,10},{5,11},{9,15},{13,14},{2,0},{6,1},... | collective-permute-start | bytes 196616 | tf_op jit(solution)/shard_map/ppermute | solution.py:296
  5.1 11.1 %collective-permute-start.2 = (bf16[128,256]{1,0:T(8,128)(2,1)S(1)}, bf16[128,256]{1,0:T(8,128)(2,1)S(1)}, u32[]{:S(2)}, u32[]{:S(2)}) collective-permute-start(bf16[128,256]{1,0:T(8,128)(2,1)S(1)} %get-tuple-element.51), channel_id=1, source_target_pairs={{0,6},{4,7},{8,3},{12,2},{1,14},{5,15},{9,11},{13,10},{2,4},{6,5},... | collective-permute-start | bytes 196616 | tf_op jit(solution)/shard_map/ppermute | solution.py:297
  11.8 31.1 %collective-permute-start = (bf16[128,896]{1,0:T(8,128)(2,1)S(1)}, bf16[128,896]{1,0:T(8,128)(2,1)S(1)}, u32[]{:S(2)}, u32[]{:S(2)}) collective-permute-start(bf16[128,896]{1,0:T(8,128)(2,1)S(1)} %get-tuple-element.49), channel_id=1, source_target_pairs={{0,2},{4,3},{8,7},{12,6},{1,10},{5,11},{9,15},{13,14},{2,0},{6,1},... | collective-permute-start | bytes 688136 | tf_op jit(solution)/shard_map/ppermute | solution.py:296
  30.7 12.4 %collective-permute-start.3 = (bf16[128,896]{1,0:T(8,128)(2,1)S(1)}, bf16[128,896]{1,0:T(8,128)(2,1)S(1)}, u32[]{:S(2)}, u32[]{:S(2)}) collective-permute-start(bf16[128,896]{1,0:T(8,128)(2,1)S(1)} %get-tuple-element.25), channel_id=1, source_target_pairs={{0,6},{4,7},{8,3},{12,2},{1,14},{5,15},{9,11},{13,10},{2,4},{6,5},... | collective-permute-start | bytes 688136 | tf_op jit(solution)/shard_map/ppermute | solution.py:297
  37.1 16.3 %collective-permute-start.5 = (bf16[512,512]{1,0:T(8,128)(2,1)S(1)}, bf16[512,512]{1,0:T(8,128)(2,1)S(1)}, u32[]{:S(2)}, u32[]{:S(2)}) collective-permute-start(bf16[512,512]{1,0:T(8,128)(2,1)S(1)} %all_gather.3.refs_0_), channel_id=1, source_target_pairs={{0,64},{1,65},{2,66},{3,67},{4,68},{5,69},{6,70},{7,71},{8,72},{9,... | collective-permute-start | bytes 1572872 | tf_op jit(solution)/shard_map/ppermute | solution.py:59
  39.0 17.8 %collective-permute-start.8 = (bf16[512,512]{1,0:T(8,128)(2,1)S(1)}, bf16[512,512]{1,0:T(8,128)(2,1)S(1)}, u32[]{:S(2)}, u32[]{:S(2)}) collective-permute-start(bf16[512,512]{1,0:T(8,128)(2,1)S(1)} %all_gather.3.refs_0_), channel_id=1, source_target_pairs={{0,448},{1,449},{2,450},{3,451},{4,452},{5,453},{6,454},{7,455},{8... | collective-permute-start | bytes 1572872 | tf_op jit(solution)/shard_map/ppermute | solution.py:59
  43.1 16.1 %collective-permute-start.4 = (bf16[2,128,896]{2,1,0:T(8,128)(2,1)S(1)}, bf16[2,128,896]{2,1,0:T(8,128)(2,1)S(1)}, u32[]{:S(2)}, u32[]{:S(2)}) collective-permute-start(bf16[2,128,896]{2,1,0:T(8,128)(2,1)S(1)} %pad_maximum_fusion.own_ref), channel_id=1, source_target_pairs={{0,1},{1,0},{2,3},{3,2},{4,5},{5,4},{6,7},{7,6},{8,9},{9,8},{10,11... | collective-permute-start | bytes 1376264 | tf_op jit(solution)/shard_map/ppermute | solution.py:318
  53.3 15.4 %collective-permute-start.6 = (bf16[512,512]{1,0:T(8,128)(2,1)S(1)}, bf16[512,512]{1,0:T(8,128)(2,1)S(1)}, u32[]{:S(2)}, u32[]{:S(2)}) collective-permute-start(bf16[512,512]{1,0:T(8,128)(2,1)S(1)} %collective-permute-done.5.refs_0_), channel_id=1, source_target_pairs={{0,64},{1,65},{2,66},{3,67},{4,68},{5,69},{6,70},{7,71},{8,72},{9,... | collective-permute-start | bytes 1572872 | tf_op jit(solution)/shard_map/ppermute | solution.py:59
  56.8 16.9 %collective-permute-start.10 = (bf16[512,512]{1,0:T(8,128)(2,1)S(1)}, bf16[512,512]{1,0:T(8,128)(2,1)S(1)}, u32[]{:S(2)}, u32[]{:S(2)}) collective-permute-start(bf16[512,512]{1,0:T(8,128)(2,1)S(1)} %collective-permute-done.8.refs_1_), channel_id=1, source_target_pairs={{0,448},{1,449},{2,450},{3,451},{4,452},{5,453},{6,454},{7,455},{8... | collective-permute-start | bytes 1572872 | tf_op jit(solution)/shard_map/ppermute | solution.py:59
  68.8 16.0 %collective-permute-start.7 = (bf16[512,512]{1,0:T(8,128)(2,1)S(1)}, bf16[512,512]{1,0:T(8,128)(2,1)S(1)}, u32[]{:S(2)}, u32[]{:S(2)}) collective-permute-start(bf16[512,512]{1,0:T(8,128)(2,1)S(1)} %collective-permute-done.6.refs_0_), channel_id=1, source_target_pairs={{0,64},{1,65},{2,66},{3,67},{4,68},{5,69},{6,70},{7,71},{8,72},{9,... | collective-permute-start | bytes 1572872 | tf_op jit(solution)/shard_map/ppermute | solution.py:59
  73.7 16.1 %collective-permute-start.11 = (bf16[512,512]{1,0:T(8,128)(2,1)S(1)}, bf16[512,512]{1,0:T(8,128)(2,1)S(1)}, u32[]{:S(2)}, u32[]{:S(2)}) collective-permute-start(bf16[512,512]{1,0:T(8,128)(2,1)S(1)} %collective-permute-done.10.refs_1_), channel_id=1, source_target_pairs={{0,448},{1,449},{2,450},{3,451},{4,452},{5,453},{6,454},{7,455},{8... | collective-permute-start | bytes 1572872 | tf_op jit(solution)/shard_map/ppermute | solution.py:59
  84.8 25.1 %collective-permute-start.9 = (bf16[256,512]{1,0:T(8,128)(2,1)S(1)}, bf16[256,512]{1,0:T(8,128)(2,1)S(1)}, u32[]{:S(2)}, u32[]{:S(2)}) collective-permute-start(bf16[256,512]{1,0:T(8,128)(2,1)S(1)} %slice.40), channel_id=1, source_target_pairs={{0,64},{1,65},{2,66},{3,67},{4,68},{5,69},{6,70},{7,71},{8,72},{9,... | collective-permute-start | bytes 786440 | tf_op jit(solution)/shard_map/ppermute | solution.py:59
  89.8 20.2 %collective-permute-start.12 = (bf16[256,512]{1,0:T(8,128)(2,1)S(1)}, bf16[256,512]{1,0:T(8,128)(2,1)S(1)}, u32[]{:S(2)}, u32[]{:S(2)}) collective-permute-start(bf16[256,512]{1,0:T(8,128)(2,1)S(1)} %slice.41), channel_id=1, source_target_pairs={{0,448},{1,449},{2,450},{3,451},{4,452},{5,453},{6,454},{7,455},{8... | collective-permute-start | bytes 786440 | tf_op jit(solution)/shard_map/ppermute | solution.py:59
  115.4 5.7 %collective-permute-start.13 = (f32[2,896,256]{2,1,0:T(8,128)S(1)}, f32[2,896,256]{2,1,0:T(8,128)S(1)}, u32[]{:S(2)}, u32[]{:S(2)}) collective-permute-start(f32[2,896,256]{2,1,0:T(8,128)S(1)} %get-tuple-element.44), channel_id=1, source_target_pairs={{0,1},{1,0},{2,3},{3,2},{4,5},{5,4},{6,7},{7,6},{8,9},{9,8},{10,11... | collective-permute-start | bytes 5505032 | tf_op jit(solution)/shard_map/ppermute | solution.py:351
  122.4 9.9 %collective-permute-start.14 = (bf16[128,896]{1,0:T(8,128)(2,1)S(1)}, bf16[128,896]{1,0:T(8,128)(2,1)S(1)}, u32[]{:S(2)}, u32[]{:S(2)}) collective-permute-start(bf16[128,896]{1,0:T(8,128)(2,1)S(1)} %get-tuple-element.47), channel_id=1, source_target_pairs={{2,0},{3,4},{7,8},{6,12},{10,1},{11,5},{15,9},{14,13},{0,2},{1,6},... | collective-permute-start | bytes 688136 | tf_op jit(solution)/shard_map/ppermute | solution.py:360
  124.7 12.2 %collective-permute-start.15 = (bf16[128,896]{1,0:T(8,128)(2,1)S(1)}, bf16[128,896]{1,0:T(8,128)(2,1)S(1)}, u32[]{:S(2)}, u32[]{:S(2)}) collective-permute-start(bf16[128,896]{1,0:T(8,128)(2,1)S(1)} %get-tuple-element.48), channel_id=1, source_target_pairs={{6,0},{7,4},{3,8},{2,12},{14,1},{15,5},{11,9},{10,13},{4,2},{5,6},... | collective-permute-start | bytes 688136 | tf_op jit(solution)/shard_map/ppermute | solution.py:361

commit v2 on v1

--- a/solution.py
+++ b/solution.py
@@ -163,13 +163,14 @@
         acc_ref[slot, rows, :] = acc_ref[slot, rows, :] * fade + product
 
 
-def attend_kernel(first, last, offsets, where_ref, query_ref, *refs):
+def attend_kernel(first, last, diagonal, offsets, where_ref, query_ref, *refs):
     number = 1 if first else len(offsets)
     block_refs = refs[:number]
     refs = refs[number:]
     if last:
-        out_refs = refs[3:5]
-        refs = refs[:3] + refs[5:]
+        send_ref = refs[6]
+        own_refs = refs[3:6]
+        refs = refs[:3] + refs[7:]
     if not first:
         for source, target in zip(refs[:3], refs[3:6]):
             target[...] = source[...]
@@ -208,7 +209,7 @@
     if first:
         column = lax.broadcasted_iota(jnp.int32, (CHUNK, SPAN), 1)
         causal(block_refs[:1], (column, x * ROWS))
-    else:
+    elif diagonal:
         for offset in sorted(set(offsets)):
 
             @pl.when(((y + offset) & (Y - 1)) < y)
@@ -216,23 +217,77 @@
                 causal([block_refs[b] for b in range(number) if offsets[b] == offset], None)
 
     if last:
-        lane = lax.broadcasted_iota(jnp.int32, (STACKED, HEAD_SIZE), 1)
-        for k in range(4):
-            ref = out_refs[k // 2]
-            total = jnp.sum(sum_ref[k], axis=-1, keepdims=True)
-            ref[k % 2, :, :HEAD_SIZE] = acc_ref[k]
-            ref[k % 2, :, HEAD_SIZE:] = jnp.where(lane < HEAD_SIZE // 2, top_ref[k], total)
-
-
-def attend(where, query, blocks, offsets, state, first=False, last=False):
+        for state, own in zip((acc_ref, top_ref, sum_ref), own_refs):
+            own[...] = state[:2]
+        pack(acc_ref, top_ref, sum_ref, 2, send_ref)
+
+
+def pack(acc_ref, top_ref, sum_ref, start, out_ref):
+    lane = lax.broadcasted_iota(jnp.int32, (STACKED, HEAD_SIZE), 1)
+    for k in range(2):
+        total = jnp.sum(sum_ref[start + k], axis=-1, keepdims=True)
+        out_ref[k, :, :HEAD_SIZE] = acc_ref[start + k]
+        out_ref[k, :, HEAD_SIZE:] = jnp.where(lane < HEAD_SIZE // 2, top_ref[start + k], total)
+
+
+def rest_kernel(groups, where_ref, query_ref, *refs):
+    y = where_ref[3]
+    count = sum(number for _, number in groups)
+    block_refs = refs[:count]
+    sources = refs[count : count + 3]
+    out_ref = refs[count + 3]
+    states = refs[count + 4 :]
+    for source, target in zip(sources, states):
+        target[...] = source[...]
+    acc_ref, top_ref, sum_ref = states
+    start = 0
+    for offset, number in groups:
+        members = block_refs[start : start + number]
+        start += number
+
+        @pl.when(((y + offset) & (Y - 1)) < y)
+        def _(members=members):
+            def body(query, carry):
+                keys = pl.multiple_of(query * (2 * HEAD_SIZE), 2 * HEAD_SIZE)
+                values = pl.multiple_of(keys + HEAD_SIZE, HEAD_SIZE)
+                pairs = [
+                    (ref[:, pl.ds(keys, HEAD_SIZE)], ref[:, pl.ds(values, HEAD_SIZE)])
+                    for ref in members
+                ]
+                absorb(query_ref, query, pairs, acc_ref, top_ref, sum_ref, query, None)
+                return carry
+
+            lax.fori_loop(0, 2, body, 0)
+
+    pack(acc_ref, top_ref, sum_ref, 0, out_ref)
+
+
+def rest(where, query, blocks, groups, state):
+    block = jax.ShapeDtypeStruct((2, STACKED, HEAD_SIZE), jnp.float32)
+    return pl.pallas_call(
+        functools.partial(rest_kernel, groups),
+        out_shape=jax.ShapeDtypeStruct((2, STACKED, 2 * HEAD_SIZE), jnp.float32),
+        in_specs=[SMEM] + [VMEM] * (1 + len(blocks) + 3),
+        out_specs=VMEM,
+        scratch_shapes=[pltpu.VMEM(block.shape, block.dtype)] * 3,
+        cost_estimate=pl.CostEstimate(
+            flops=12 * STACKED * SPAN * HEAD_SIZE, bytes_accessed=4 << 20, transcendentals=0
+        ),
+        compiler_params=pltpu.CompilerParams(vmem_limit_bytes=20 << 20),
+        name="rest",
+    )(where, query, *blocks, *state)
+
+
+def attend(where, query, blocks, offsets, state, first=False, last=False, diagonal=True):
     number = len(blocks)
     block = jax.ShapeDtypeStruct((4, STACKED, HEAD_SIZE), jnp.float32)
     outs = [block] * 3
     if last:
-        outs = [jax.ShapeDtypeStruct((2, STACKED, 2 * HEAD_SIZE), jnp.float32)] * 2
+        outs = [jax.ShapeDtypeStruct((2, STACKED, HEAD_SIZE), jnp.float32)] * 3
+        outs.append(jax.ShapeDtypeStruct((2, STACKED, 2 * HEAD_SIZE), jnp.float32))
     flops = number * 4 * 4 * STACKED * SPAN * HEAD_SIZE
     return pl.pallas_call(
-        functools.partial(attend_kernel, first, last, offsets),
+        functools.partial(attend_kernel, first, last, diagonal, offsets),
         out_shape=outs,
         in_specs=[SMEM] + [VMEM] * (1 + number + len(state)),
         out_specs=[VMEM] * len(outs),
@@ -340,15 +395,23 @@
     step(1, None)
     step(2, None)
     for hop in range(Y // 2):
+        before = states[-1] if states else []
         states.append(
             attend(
-                base, query, rounds[hop], (-hop, hop), states[-1] if states else [], first=hop == 0
+                base,
+                query,
+                rounds[hop],
+                (-hop, hop),
+                before,
+                first=hop == 0,
+                diagonal=hop < 3,
             )
         )
-        if hop < 2:
-            step(hop + 3, states[-1][2])
-    mine, send = attend(base, query, rounds[4], (4, 4), states[-1], last=True)
+        if hop in (1, 2):
+            step(hop + 2, states[-1][2])
+    *kept, send = attend(base, query, rounds[4], (4, 4), states[-1], last=True, diagonal=False)
     received = lax.ppermute(send, "stretch", SWAP)
+    mine = rest(base, query, [*rounds[3], *rounds[4]], ((-3, 1), (3, 1), (4, 2)), kept)
     merged = pl.pallas_call(
         merge_kernel,
         out_shape=jax.ShapeDtypeStruct((2, ROWS, half), jnp.bfloat16),

time: 140 us -> 139 us (level)
  waiting for transfers between devices: 21.8 us -> 17.9 us
  starting transfers between devices: 56.7 us -> 59 us
    ppermute x1, waiting for transfers between devices: 3.75 us -> 0.01 us  [on_device(): received = lax.ppermute(send, 'stretch', SWAP)]
    ppermute x8, starting transfers between devices: 25.3 us -> 28.4 us  [shifted(): return lax.ppermute(array, ('seq', 'stretch'), plane_shift(dx, dy))]
    ppermute x1, waiting for transfers between devices: 4.62 us -> 7.69 us  [on_device(): two = lax.ppermute(merged[1], 'stretch', back(crossed))]
    ppermute x8, waiting for transfers between devices: 8.45 us -> 6.56 us  [shifted(): return lax.ppermute(array, ('seq', 'stretch'), plane_shift(dx, dy))]
    pallas_call x5 -> x6, Pallas kernels: 38.2 us -> 38.5 us  [the longest x5 32.3 us: attend(): pl.pallas_call(functools.partial(attend_kernel, first, last, diagonal, of...]
  transfers between devices with their start and end apart: 16 -> 16, of which waited for: 7 -> 4; matrix products, arithmetic and copies ran while one was open for 2% -> 2% of each run, Pallas kernels for 25% -> 27%
where the time goes in v2:
time: 139 us; the launch traced here: 137 us
  starting transfers between devices  59 us (42%)
  Pallas kernels  41.5 us (30%)
  waiting for transfers between devices  17.9 us (13%)
  blocking collectives  13.8 us (10%)
  other arithmetic  2.99 us (2%)
    pallas_call x5, Pallas kernels, attend(): pl.pallas_call(functools.partial(attend_kernel, first, last, diagonal, of...  32.3 us
    ppermute x8, starting transfers between devices, shifted(): return lax.ppermute(array, ('seq', 'stretch'), plane_shift(dx, dy))  28.4 us
    all_gather x1, blocking collectives, on_device(): lax.all_gather(own, 'seq', axis=0, tiled=True, axis_index_groups=lines)  13.8 us
    ppermute x2, starting transfers between devices, spread(): two = lax.ppermute(second, 'stretch', crossed)  11.9 us
    ppermute x1, waiting for transfers between devices, on_device(): two = lax.ppermute(merged[1], 'stretch', back(crossed))  7.69 us
    ppermute x8, waiting for transfers between devices, shifted(): return lax.ppermute(array, ('seq', 'stretch'), plane_shift(dx, dy))  6.56 us
    ppermute x2, starting transfers between devices, spread(): one = lax.ppermute(first, 'stretch', straight)  6.2 us
    pallas_call x1, Pallas kernels, rest(): pl.pallas_call(functools.partial(rest_kernel, groups), out_shape=jax.Shap...  6.2 us
  transfers between devices with their start and end apart: 16, of which 4 were waited for; matrix products, arithmetic and copies ran while one was open for 2% of the time, Pallas kernels for 27%

profile of v2, /device:TPU:56, one launch (start us, length us, event | category | flops | bytes accessed | tf_op | source)
XLA Modules:
  0.0 136.5 jit_solution(5402843074953210744)
XLA Ops:
  0.0 0.8 fusion.5
  0.9 4.3 %collective-permute-start.1 = (bf16[128,256]{1,0:T(8,128)(2,1)S(1)}, bf16[128,256]{1,0:T(8,128)(2,1)S(1)}, u32[]{:S(2)}, u32[]{:S(2)}) collective-permute-start(bf16[128,256]{1,0:T(8,128)(2,1)S(1)} %get-tuple-element.56), channel_id=1, source_target_pairs={{0,2},{4,3},{8,7},{12,6},{1,10},{5,11},{9,15},{13,14},{2,0},{6,1},... | collective-permute-start | bytes 196616 | tf_op jit(solution)/shard_map/ppermute | solution.py:351
  5.1 5.5 %collective-permute-start.2 = (bf16[128,256]{1,0:T(8,128)(2,1)S(1)}, bf16[128,256]{1,0:T(8,128)(2,1)S(1)}, u32[]{:S(2)}, u32[]{:S(2)}) collective-permute-start(bf16[128,256]{1,0:T(8,128)(2,1)S(1)} %get-tuple-element.55), channel_id=1, source_target_pairs={{0,6},{4,7},{8,3},{12,2},{1,14},{5,15},{9,11},{13,10},{2,4},{6,5},... | collective-permute-start | bytes 196616 | tf_op jit(solution)/shard_map/ppermute | solution.py:352
  10.7 1.1 broadcast_select_fusion.3
  11.8 1.9 %collective-permute-start = (bf16[128,896]{1,0:T(8,128)(2,1)S(1)}, bf16[128,896]{1,0:T(8,128)(2,1)S(1)}, u32[]{:S(2)}, u32[]{:S(2)}) collective-permute-start(bf16[128,896]{1,0:T(8,128)(2,1)S(1)} %get-tuple-element.53), channel_id=1, source_target_pairs={{0,2},{4,3},{8,7},{12,6},{1,10},{5,11},{9,15},{13,14},{2,0},{6,1},... | collective-permute-start | bytes 688136 | tf_op jit(solution)/shard_map/ppermute | solution.py:351
  14.8 1.5 %collective-permute-done.2.two_ref = bf16[128,256]{1,0:T(8,128)(2,1)S(1)} collective-permute-done((bf16[128,256]{1,0:T(8,128)(2,1)S(1)}, bf16[128,256]{1,0:T(8,128)(2,1)S(1)}, u32[]{:S(2)}, u32[]{:S(2)}) %collective-permute-start.2) | collective-permute-done | bytes 65568 | tf_op jit(solution)/shard_map/ppermute | solution.py:352
  16.9 13.8 %all_gather.3.refs_0_ = bf16[512,512]{1,0:T(8,128)(2,1)S(1)} all-gather(bf16[128,512]{1,0:T(8,128)(2,1)S(1)} %turn_keys.1), channel_id=1, replica_groups={{0,16,32,48},{64,80,96,112},{128,144,160,176},{192,208,224,240},{256,27..., dimensions={0}, use_global_device_ids=true | all-gather | bytes 655360 | tf_op jit(solution)/shard_map/all_gather | solution.py:369
  30.7 6.4 %collective-permute-start.3 = (bf16[128,896]{1,0:T(8,128)(2,1)S(1)}, bf16[128,896]{1,0:T(8,128)(2,1)S(1)}, u32[]{:S(2)}, u32[]{:S(2)}) collective-permute-start(bf16[128,896]{1,0:T(8,128)(2,1)S(1)} %get-tuple-element.27), channel_id=1, source_target_pairs={{0,6},{4,7},{8,3},{12,2},{1,14},{5,15},{9,11},{13,10},{2,4},{6,5},... | collective-permute-start | bytes 688136 | tf_op jit(solution)/shard_map/ppermute | solution.py:352
  37.1 3.3 %collective-permute-start.7 = (bf16[512,512]{1,0:T(8,128)(2,1)S(1)}, bf16[512,512]{1,0:T(8,128)(2,1)S(1)}, u32[]{:S(2)}, u32[]{:S(2)}) collective-permute-start(bf16[512,512]{1,0:T(8,128)(2,1)S(1)} %all_gather.3.refs_0_), channel_id=1, source_target_pairs={{0,448},{1,449},{2,450},{3,451},{4,452},{5,453},{6,454},{7,455},{8... | collective-permute-start | bytes 1572872 | tf_op jit(solution)/shard_map/ppermute | solution.py:59
  40.3 3.8 %collective-permute-start.5 = (bf16[512,512]{1,0:T(8,128)(2,1)S(1)}, bf16[512,512]{1,0:T(8,128)(2,1)S(1)}, u32[]{:S(2)}, u32[]{:S(2)}) collective-permute-start(bf16[512,512]{1,0:T(8,128)(2,1)S(1)} %all_gather.3.refs_0_), channel_id=1, source_target_pairs={{0,64},{1,65},{2,66},{3,67},{4,68},{5,69},{6,70},{7,71},{8,72},{9,... | collective-permute-start | bytes 1572872 | tf_op jit(solution)/shard_map/ppermute | solution.py:59
  44.2 3.8 %collective-permute-start.4 = (bf16[2,128,896]{2,1,0:T(8,128)(2,1)S(1)}, bf16[2,128,896]{2,1,0:T(8,128)(2,1)S(1)}, u32[]{:S(2)}, u32[]{:S(2)}) collective-permute-start(bf16[2,128,896]{2,1,0:T(8,128)(2,1)S(1)} %pad_maximum_fusion.own_ref), channel_id=1, source_target_pairs={{0,1},{1,0},{2,3},{3,2},{4,5},{5,4},{6,7},{7,6},{8,9},{9,8},{10,11... | collective-permute-start | bytes 1376264 | tf_op jit(solution)/shard_map/ppermute | solution.py:373
  48.0 6.5 %collective-permute-done.7.refs_1_ = bf16[512,512]{1,0:T(8,128)(2,1)S(1)} collective-permute-done((bf16[512,512]{1,0:T(8,128)(2,1)S(1)}, bf16[512,512]{1,0:T(8,128)(2,1)S(1)}, u32[]{:S(2)}, u32[]{:S(2)}) %collective-permute-start.7) | collective-permute-done | bytes 524320 | tf_op jit(solution)/shard_map/ppermute | solution.py:59
  54.6 2.0 %collective-permute-start.9 = (bf16[512,512]{1,0:T(8,128)(2,1)S(1)}, bf16[512,512]{1,0:T(8,128)(2,1)S(1)}, u32[]{:S(2)}, u32[]{:S(2)}) collective-permute-start(bf16[512,512]{1,0:T(8,128)(2,1)S(1)} %collective-permute-done.7.refs_1_), channel_id=1, source_target_pairs={{0,448},{1,449},{2,450},{3,451},{4,452},{5,453},{6,454},{7,455},{8... | collective-permute-start | bytes 1572872 | tf_op jit(solution)/shard_map/ppermute | solution.py:59
  56.6 5.0 %collective-permute-start.6 = (bf16[512,512]{1,0:T(8,128)(2,1)S(1)}, bf16[512,512]{1,0:T(8,128)(2,1)S(1)}, u32[]{:S(2)}, u32[]{:S(2)}) collective-permute-start(bf16[512,512]{1,0:T(8,128)(2,1)S(1)} %collective-permute-done.5.refs_0_), channel_id=1, source_target_pairs={{0,64},{1,65},{2,66},{3,67},{4,68},{5,69},{6,70},{7,71},{8,72},{9,... | collective-permute-start | bytes 1572872 | tf_op jit(solution)/shard_map/ppermute | solution.py:59
  61.6 1.1 turn_queries.1.query_ref
  62.8 5.3 %attend.5 = (f32[4,896,128]{2,1,0:T(8,128)S(1)}, f32[4,896,128]{2,1,0:T(8,128)S(1)}, f32[4,896,128]{2,1,0:T(8,128)S(1)}) custom-call(s32[4]{0:T(128)S(1)} %pad_add_fusion.where_ref, bf16[5,896,128]{2,1,0:T(8,128)(2,1)S(1)} %turn_queries.1.query_ref, bf16[512,512]{1,0:T(8,128)(2,1)S(1)} %all_gather.3.refs_0_), custom_call_target="tpu_custom_call" | custom-call | flops 939524096 | bytes 4194304 | tf_op jit(solution)/shard_map/attend/pallas_call | solution.py:289
  68.1 9.2 %attend.6 = (f32[4,896,128]{2,1,0:T(8,128)S(1)}, f32[4,896,128]{2,1,0:T(8,128)S(1)}, f32[4,896,128]{2,1,0:T(8,128)S(1)}) custom-call(s32[4]{0:T(128)S(1)} %pad_add_fusion.where_ref, bf16[5,896,128]{2,1,0:T(8,128)(2,1)S(1)} %turn_queries.1.query_ref, bf16[512,512]{1,0:T(8,128)(2,1)S(1)} %collective-permute-done.5.refs_0_, ...), custom_call_target="tpu_custom_call" | custom-call | flops 1879048192 | bytes 4194304 | tf_op jit(solution)/shard_map/attend/pallas_call | solution.py:289
  77.2 1.9 %collective-permute-start.10 = (bf16[512,512]{1,0:T(8,128)(2,1)S(1)}, bf16[512,512]{1,0:T(8,128)(2,1)S(1)}, u32[]{:S(2)}, u32[]{:S(2)}) collective-permute-start(bf16[512,512]{1,0:T(8,128)(2,1)S(1)} %collective-permute-done.9.refs_1_), channel_id=1, source_target_pairs={{0,448},{1,449},{2,450},{3,451},{4,452},{5,453},{6,454},{7,455},{8... | collective-permute-start | bytes 1572872 | tf_op jit(solution)/shard_map/ppermute | solution.py:59
  79.2 5.1 %collective-permute-start.8 = (bf16[512,512]{1,0:T(8,128)(2,1)S(1)}, bf16[512,512]{1,0:T(8,128)(2,1)S(1)}, u32[]{:S(2)}, u32[]{:S(2)}) collective-permute-start(bf16[512,512]{1,0:T(8,128)(2,1)S(1)} %collective-permute-done.6.refs_0_), channel_id=1, source_target_pairs={{0,64},{1,65},{2,66},{3,67},{4,68},{5,69},{6,70},{7,71},{8,72},{9,... | collective-permute-start | bytes 1572872 | tf_op jit(solution)/shard_map/ppermute | solution.py:59
  84.3 9.0 %attend.7 = (f32[4,896,128]{2,1,0:T(8,128)S(1)}, f32[4,896,128]{2,1,0:T(8,128)S(1)}, f32[4,896,128]{2,1,0:T(8,128)S(1)}) custom-call(s32[4]{0:T(128)S(1)} %pad_add_fusion.where_ref, bf16[5,896,128]{2,1,0:T(8,128)(2,1)S(1)} %turn_queries.1.query_ref, bf16[512,512]{1,0:T(8,128)(2,1)S(1)} %collective-permute-done.6.refs_0_, ...), custom_call_target="tpu_custom_call" | custom-call | flops 1879048192 | bytes 4194304 | tf_op jit(solution)/shard_map/attend/pallas_call | solution.py:289
  93.4 1.9 %collective-permute-start.12 = (bf16[256,512]{1,0:T(8,128)(2,1)S(1)}, bf16[256,512]{1,0:T(8,128)(2,1)S(1)}, u32[]{:S(2)}, u32[]{:S(2)}) collective-permute-start(bf16[256,512]{1,0:T(8,128)(2,1)S(1)} %slice.41), channel_id=1, source_target_pairs={{0,448},{1,449},{2,450},{3,451},{4,452},{5,453},{6,454},{7,455},{8... | collective-permute-start | bytes 786440 | tf_op jit(solution)/shard_map/ppermute | solution.py:59
  95.3 5.4 %collective-permute-start.11 = (bf16[256,512]{1,0:T(8,128)(2,1)S(1)}, bf16[256,512]{1,0:T(8,128)(2,1)S(1)}, u32[]{:S(2)}, u32[]{:S(2)}) collective-permute-start(bf16[256,512]{1,0:T(8,128)(2,1)S(1)} %slice.40), channel_id=1, source_target_pairs={{0,64},{1,65},{2,66},{3,67},{4,68},{5,69},{6,70},{7,71},{8,72},{9,... | collective-permute-start | bytes 786440 | tf_op jit(solution)/shard_map/ppermute | solution.py:59
  100.7 5.3 %attend.8 = (f32[4,896,128]{2,1,0:T(8,128)S(1)}, f32[4,896,128]{2,1,0:T(8,128)S(1)}, f32[4,896,128]{2,1,0:T(8,128)S(1)}) custom-call(s32[4]{0:T(128)S(1)} %pad_add_fusion.where_ref, bf16[5,896,128]{2,1,0:T(8,128)(2,1)S(1)} %turn_queries.1.query_ref, bf16[512,512]{1,0:T(8,128)(2,1)S(1)} %collective-permute-done.8.refs_0_, ...), custom_call_target="tpu_custom_call" | custom-call | flops 1879048192 | bytes 4194304 | tf_op jit(solution)/shard_map/attend/pallas_call | solution.py:289
  106.1 3.5 %attend.9 = (f32[2,896,128]{2,1,0:T(8,128)S(1)}, f32[2,896,128]{2,1,0:T(8,128)S(1)}, f32[2,896,128]{2,1,0:T(8,128)S(1)}, f32[2,896,256]{2,1,0:T(8,128)S(1)}) custom-call(s32[4]{0:T(128)S(1)} %pad_add_fusion.where_ref, bf16[5,896,128]{2,1,0:T(8,128)(2,1)S(1)} %turn_queries.1.query_ref, bf16[256,512]{1,0:T(8,128)(2,1)S(1)} %collective-permute-done.11.refs_0_.refs_2_, ...), custom_call_target="tpu_custom_call" | custom-call | flops 1879048192 | bytes 4194304 | tf_op jit(solution)/shard_map/attend/pallas_call | solution.py:289
  109.5 1.9 %collective-permute-start.13 = (f32[2,896,256]{2,1,0:T(8,128)S(1)}, f32[2,896,256]{2,1,0:T(8,128)S(1)}, u32[]{:S(2)}, u32[]{:S(2)}) collective-permute-start(f32[2,896,256]{2,1,0:T(8,128)S(1)} %get-tuple-element.48), channel_id=1, source_target_pairs={{0,1},{1,0},{2,3},{3,2},{4,5},{5,4},{6,7},{7,6},{8,9},{9,8},{10,11... | collective-permute-start | bytes 5505032 | tf_op jit(solution)/shard_map/ppermute | solution.py:413
  111.5 6.2 %rest.1.own_ref = f32[2,896,256]{2,1,0:T(8,128)S(1)} custom-call(s32[4]{0:T(128)S(1)} %pad_add_fusion.where_ref, bf16[5,896,128]{2,1,0:T(8,128)(2,1)S(1)} %turn_queries.1.query_ref, bf16[512,512]{1,0:T(8,128)(2,1)S(1)} %collective-permute-done.8.refs_0_, bf16[512,512]{1,0:T(8,128)(2,1)S(1)} %collective-permute-done.10.refs_1_, ...), custom_call_target="tpu_custom_call" | custom-call | flops 704643072 | bytes 4194304 | tf_op jit(solution)/shard_map/rest/pallas_call | solution.py:267
  117.7 1.3 merge.1
  119.0 2.9 %collective-permute-start.14 = (bf16[128,896]{1,0:T(8,128)(2,1)S(1)}, bf16[128,896]{1,0:T(8,128)(2,1)S(1)}, u32[]{:S(2)}, u32[]{:S(2)}) collective-permute-start(bf16[128,896]{1,0:T(8,128)(2,1)S(1)} %get-tuple-element.51), channel_id=1, source_target_pairs={{2,0},{3,4},{7,8},{6,12},{10,1},{11,5},{15,9},{14,13},{0,2},{1,6},... | collective-permute-start | bytes 688136 | tf_op jit(solution)/shard_map/ppermute | solution.py:423
  121.9 3.9 %collective-permute-start.15 = (bf16[128,896]{1,0:T(8,128)(2,1)S(1)}, bf16[128,896]{1,0:T(8,128)(2,1)S(1)}, u32[]{:S(2)}, u32[]{:S(2)}) collective-permute-start(bf16[128,896]{1,0:T(8,128)(2,1)S(1)} %get-tuple-element.52), channel_id=1, source_target_pairs={{6,0},{7,4},{3,8},{2,12},{14,1},{15,5},{11,9},{10,13},{4,2},{5,6},... | collective-permute-start | bytes 688136 | tf_op jit(solution)/shard_map/ppermute | solution.py:424
  125.8 2.2 %collective-permute-done.14 = bf16[128,896]{1,0:T(8,128)(2,1)S(1)} collective-permute-done((bf16[128,896]{1,0:T(8,128)(2,1)S(1)}, bf16[128,896]{1,0:T(8,128)(2,1)S(1)}, u32[]{:S(2)}, u32[]{:S(2)}) %collective-permute-start.14) | collective-permute-done | bytes 229408 | tf_op jit(solution)/shard_map/ppermute | solution.py:423
  128.0 7.7 %collective-permute-done.15 = bf16[128,896]{1,0:T(8,128)(2,1)S(1)} collective-permute-done((bf16[128,896]{1,0:T(8,128)(2,1)S(1)}, bf16[128,896]{1,0:T(8,128)(2,1)S(1)}, u32[]{:S(2)}, u32[]{:S(2)}) %collective-permute-start.15) | collective-permute-done | bytes 229408 | tf_op jit(solution)/shard_map/ppermute | solution.py:424
  135.7 0.8 pad_maximum_fusion.1
  (27 shorter events, 1.8 us)
Async XLA Ops:
  0.9 13.9 %collective-permute-start.1 = (bf16[128,256]{1,0:T(8,128)(2,1)S(1)}, bf16[128,256]{1,0:T(8,128)(2,1)S(1)}, u32[]{:S(2)}, u32[]{:S(2)}) collective-permute-start(bf16[128,256]{1,0:T(8,128)(2,1)S(1)} %get-tuple-element.56), channel_id=1, source_target_pairs={{0,2},{4,3},{8,7},{12,6},{1,10},{5,11},{9,15},{13,14},{2,0},{6,1},... | collective-permute-start | bytes 196616 | tf_op jit(solution)/shard_map/ppermute | solution.py:351
  5.1 11.1 %collective-permute-start.2 = (bf16[128,256]{1,0:T(8,128)(2,1)S(1)}, bf16[128,256]{1,0:T(8,128)(2,1)S(1)}, u32[]{:S(2)}, u32[]{:S(2)}) collective-permute-start(bf16[128,256]{1,0:T(8,128)(2,1)S(1)} %get-tuple-element.55), channel_id=1, source_target_pairs={{0,6},{4,7},{8,3},{12,2},{1,14},{5,15},{9,11},{13,10},{2,4},{6,5},... | collective-permute-start | bytes 196616 | tf_op jit(solution)/shard_map/ppermute | solution.py:352
  11.8 32.4 %collective-permute-start = (bf16[128,896]{1,0:T(8,128)(2,1)S(1)}, bf16[128,896]{1,0:T(8,128)(2,1)S(1)}, u32[]{:S(2)}, u32[]{:S(2)}) collective-permute-start(bf16[128,896]{1,0:T(8,128)(2,1)S(1)} %get-tuple-element.53), channel_id=1, source_target_pairs={{0,2},{4,3},{8,7},{12,6},{1,10},{5,11},{9,15},{13,14},{2,0},{6,1},... | collective-permute-start | bytes 688136 | tf_op jit(solution)/shard_map/ppermute | solution.py:351
  30.7 13.5 %collective-permute-start.3 = (bf16[128,896]{1,0:T(8,128)(2,1)S(1)}, bf16[128,896]{1,0:T(8,128)(2,1)S(1)}, u32[]{:S(2)}, u32[]{:S(2)}) collective-permute-start(bf16[128,896]{1,0:T(8,128)(2,1)S(1)} %get-tuple-element.27), channel_id=1, source_target_pairs={{0,6},{4,7},{8,3},{12,2},{1,14},{5,15},{9,11},{13,10},{2,4},{6,5},... | collective-permute-start | bytes 688136 | tf_op jit(solution)/shard_map/ppermute | solution.py:352
  37.1 17.5 %collective-permute-start.7 = (bf16[512,512]{1,0:T(8,128)(2,1)S(1)}, bf16[512,512]{1,0:T(8,128)(2,1)S(1)}, u32[]{:S(2)}, u32[]{:S(2)}) collective-permute-start(bf16[512,512]{1,0:T(8,128)(2,1)S(1)} %all_gather.3.refs_0_), channel_id=1, source_target_pairs={{0,448},{1,449},{2,450},{3,451},{4,452},{5,453},{6,454},{7,455},{8... | collective-permute-start | bytes 1572872 | tf_op jit(solution)/shard_map/ppermute | solution.py:59
  40.3 16.3 %collective-permute-start.5 = (bf16[512,512]{1,0:T(8,128)(2,1)S(1)}, bf16[512,512]{1,0:T(8,128)(2,1)S(1)}, u32[]{:S(2)}, u32[]{:S(2)}) collective-permute-start(bf16[512,512]{1,0:T(8,128)(2,1)S(1)} %all_gather.3.refs_0_), channel_id=1, source_target_pairs={{0,64},{1,65},{2,66},{3,67},{4,68},{5,69},{6,70},{7,71},{8,72},{9,... | collective-permute-start | bytes 1572872 | tf_op jit(solution)/shard_map/ppermute | solution.py:59
  44.2 17.4 %collective-permute-start.4 = (bf16[2,128,896]{2,1,0:T(8,128)(2,1)S(1)}, bf16[2,128,896]{2,1,0:T(8,128)(2,1)S(1)}, u32[]{:S(2)}, u32[]{:S(2)}) collective-permute-start(bf16[2,128,896]{2,1,0:T(8,128)(2,1)S(1)} %pad_maximum_fusion.own_ref), channel_id=1, source_target_pairs={{0,1},{1,0},{2,3},{3,2},{4,5},{5,4},{6,7},{7,6},{8,9},{9,8},{10,11... | collective-permute-start | bytes 1376264 | tf_op jit(solution)/shard_map/ppermute | solution.py:373
  54.6 22.7 %collective-permute-start.9 = (bf16[512,512]{1,0:T(8,128)(2,1)S(1)}, bf16[512,512]{1,0:T(8,128)(2,1)S(1)}, u32[]{:S(2)}, u32[]{:S(2)}) collective-permute-start(bf16[512,512]{1,0:T(8,128)(2,1)S(1)} %collective-permute-done.7.refs_1_), channel_id=1, source_target_pairs={{0,448},{1,449},{2,450},{3,451},{4,452},{5,453},{6,454},{7,455},{8... | collective-permute-start | bytes 1572872 | tf_op jit(solution)/shard_map/ppermute | solution.py:59
  56.6 22.6 %collective-permute-start.6 = (bf16[512,512]{1,0:T(8,128)(2,1)S(1)}, bf16[512,512]{1,0:T(8,128)(2,1)S(1)}, u32[]{:S(2)}, u32[]{:S(2)}) collective-permute-start(bf16[512,512]{1,0:T(8,128)(2,1)S(1)} %collective-permute-done.5.refs_0_), channel_id=1, source_target_pairs={{0,64},{1,65},{2,66},{3,67},{4,68},{5,69},{6,70},{7,71},{8,72},{9,... | collective-permute-start | bytes 1572872 | tf_op jit(solution)/shard_map/ppermute | solution.py:59
  77.2 16.1 %collective-permute-start.10 = (bf16[512,512]{1,0:T(8,128)(2,1)S(1)}, bf16[512,512]{1,0:T(8,128)(2,1)S(1)}, u32[]{:S(2)}, u32[]{:S(2)}) collective-permute-start(bf16[512,512]{1,0:T(8,128)(2,1)S(1)} %collective-permute-done.9.refs_1_), channel_id=1, source_target_pairs={{0,448},{1,449},{2,450},{3,451},{4,452},{5,453},{6,454},{7,455},{8... | collective-permute-start | bytes 1572872 | tf_op jit(solution)/shard_map/ppermute | solution.py:59
  79.2 16.1 %collective-permute-start.8 = (bf16[512,512]{1,0:T(8,128)(2,1)S(1)}, bf16[512,512]{1,0:T(8,128)(2,1)S(1)}, u32[]{:S(2)}, u32[]{:S(2)}) collective-permute-start(bf16[512,512]{1,0:T(8,128)(2,1)S(1)} %collective-permute-done.6.refs_0_), channel_id=1, source_target_pairs={{0,64},{1,65},{2,66},{3,67},{4,68},{5,69},{6,70},{7,71},{8,72},{9,... | collective-permute-start | bytes 1572872 | tf_op jit(solution)/shard_map/ppermute | solution.py:59
  93.4 12.7 %collective-permute-start.12 = (bf16[256,512]{1,0:T(8,128)(2,1)S(1)}, bf16[256,512]{1,0:T(8,128)(2,1)S(1)}, u32[]{:S(2)}, u32[]{:S(2)}) collective-permute-start(bf16[256,512]{1,0:T(8,128)(2,1)S(1)} %slice.41), channel_id=1, source_target_pairs={{0,448},{1,449},{2,450},{3,451},{4,452},{5,453},{6,454},{7,455},{8... | collective-permute-start | bytes 786440 | tf_op jit(solution)/shard_map/ppermute | solution.py:59
  95.3 10.7 %collective-permute-start.11 = (bf16[256,512]{1,0:T(8,128)(2,1)S(1)}, bf16[256,512]{1,0:T(8,128)(2,1)S(1)}, u32[]{:S(2)}, u32[]{:S(2)}) collective-permute-start(bf16[256,512]{1,0:T(8,128)(2,1)S(1)} %slice.40), channel_id=1, source_target_pairs={{0,64},{1,65},{2,66},{3,67},{4,68},{5,69},{6,70},{7,71},{8,72},{9,... | collective-permute-start | bytes 786440 | tf_op jit(solution)/shard_map/ppermute | solution.py:59
  109.5 8.1 %collective-permute-start.13 = (f32[2,896,256]{2,1,0:T(8,128)S(1)}, f32[2,896,256]{2,1,0:T(8,128)S(1)}, u32[]{:S(2)}, u32[]{:S(2)}) collective-permute-start(f32[2,896,256]{2,1,0:T(8,128)S(1)} %get-tuple-element.48), channel_id=1, source_target_pairs={{0,1},{1,0},{2,3},{3,2},{4,5},{5,4},{6,7},{7,6},{8,9},{9,8},{10,11... | collective-permute-start | bytes 5505032 | tf_op jit(solution)/shard_map/ppermute | solution.py:413
  119.0 9.0 %collective-permute-start.14 = (bf16[128,896]{1,0:T(8,128)(2,1)S(1)}, bf16[128,896]{1,0:T(8,128)(2,1)S(1)}, u32[]{:S(2)}, u32[]{:S(2)}) collective-permute-start(bf16[128,896]{1,0:T(8,128)(2,1)S(1)} %get-tuple-element.51), channel_id=1, source_target_pairs={{2,0},{3,4},{7,8},{6,12},{10,1},{11,5},{15,9},{14,13},{0,2},{1,6},... | collective-permute-start | bytes 688136 | tf_op jit(solution)/shard_map/ppermute | solution.py:423
  121.9 13.8 %collective-permute-start.15 = (bf16[128,896]{1,0:T(8,128)(2,1)S(1)}, bf16[128,896]{1,0:T(8,128)(2,1)S(1)}, u32[]{:S(2)}, u32[]{:S(2)}) collective-permute-start(bf16[128,896]{1,0:T(8,128)(2,1)S(1)} %get-tuple-element.52), channel_id=1, source_target_pairs={{6,0},{7,4},{3,8},{2,12},{14,1},{15,5},{11,9},{10,13},{4,2},{5,6},... | collective-permute-start | bytes 688136 | tf_op jit(solution)/shard_map/ppermute | solution.py:424

commit v3 on v2

--- a/solution.py
+++ b/solution.py
@@ -368,8 +368,8 @@
     lines = [[X * line + k for k in range(X)] for line in range(Y)]
     row = lax.all_gather(own, "seq", axis=0, tiled=True, axis_index_groups=lines)
     straight_half, crossed_half = halves_of(queries[:, :half], queries[:, half:])
-    row, crossed_half = lax.optimization_barrier((row, crossed_half))
-    raw = jnp.stack(spread(straight_half, crossed_half))
+    row, *arrived = lax.optimization_barrier((row, *spread(straight_half, crossed_half)))
+    raw = jnp.stack(arrived)
     other_raw = lax.ppermute(raw, "stretch", SWAP)
     query = pl.pallas_call(
         query_kernel,
@@ -393,7 +393,6 @@
         rounds.append((shifted(up, 0, 1), shifted(down, 0, -1)))
 
     step(1, None)
-    step(2, None)
     for hop in range(Y // 2):
         before = states[-1] if states else []
         states.append(
@@ -407,7 +406,7 @@
                 diagonal=hop < 3,
             )
         )
-        if hop in (1, 2):
+        if hop < 3:
             step(hop + 2, states[-1][2])
     *kept, send = attend(base, query, rounds[4], (4, 4), states[-1], last=True, diagonal=False)
     received = lax.ppermute(send, "stretch", SWAP)

time: 139 us -> 136 us (0.978)
    ppermute x1, waiting for transfers between devices: 2.16 us -> 4.66 us  [on_device(): one = lax.ppermute(merged[0], 'stretch', back(straight))]
    ppermute x8, waiting for transfers between devices: 6.56 us -> 4.26 us  [shifted(): return lax.ppermute(array, ('seq', 'stretch'), plane_shift(dx, dy))]
    ppermute x2, starting transfers between devices: 11.9 us -> 14 us  [spread(): two = lax.ppermute(second, 'stretch', crossed)]
    ppermute x1, starting transfers between devices: 3.78 us -> 1.92 us  [on_device(): other_raw = lax.ppermute(raw, 'stretch', SWAP)]
    ppermute x2, waiting for transfers between devices: 1.45 us -> 0.01 us  [spread(): two = lax.ppermute(second, 'stretch', crossed)]
where the time goes in v3:
time: 136 us; the launch traced here: 135 us
  starting transfers between devices  58 us (43%)
  Pallas kernels  41.5 us (31%)
  waiting for transfers between devices  17.3 us (13%)
  blocking collectives  13.8 us (10%)
  other arithmetic  2.99 us (2%)
    pallas_call x5, Pallas kernels, attend(): pl.pallas_call(functools.partial(attend_kernel, first, last, diagonal, of...  32.3 us
    ppermute x8, starting transfers between devices, shifted(): return lax.ppermute(array, ('seq', 'stretch'), plane_shift(dx, dy))  28.4 us
    ppermute x2, starting transfers between devices, spread(): two = lax.ppermute(second, 'stretch', crossed)  14 us
    all_gather x1, blocking collectives, on_device(): lax.all_gather(own, 'seq', axis=0, tiled=True, axis_index_groups=lines)  13.8 us
    ppermute x1, waiting for transfers between devices, on_device(): two = lax.ppermute(merged[1], 'stretch', back(crossed))  8.34 us
    ppermute x2, starting transfers between devices, spread(): one = lax.ppermute(first, 'stretch', straight)  6.2 us
    pallas_call x1, Pallas kernels, rest(): pl.pallas_call(functools.partial(rest_kernel, groups), out_shape=jax.Shap...  6.2 us
    ppermute x1, waiting for transfers between devices, on_device(): one = lax.ppermute(merged[0], 'stretch', back(straight))  4.66 us
  transfers between devices with their start and end apart: 16, of which 4 were waited for; matrix products, arithmetic and copies ran while one was open for 2% of the time, Pallas kernels for 27%

profile of v3, /device:TPU:56, one launch (start us, length us, event | category | flops | bytes accessed | tf_op | source)
XLA Modules:
  0.0 134.9 jit_solution(18358641364990583773)
XLA Ops:
  0.0 0.8 fusion.5
  0.9 4.3 %collective-permute-start = (bf16[128,256]{1,0:T(8,128)(2,1)S(1)}, bf16[128,256]{1,0:T(8,128)(2,1)S(1)}, u32[]{:S(2)}, u32[]{:S(2)}) collective-permute-start(bf16[128,256]{1,0:T(8,128)(2,1)S(1)} %get-tuple-element.62), channel_id=1, source_target_pairs={{0,2},{4,3},{8,7},{12,6},{1,10},{5,11},{9,15},{13,14},{2,0},{6,1},... | collective-permute-start | bytes 196616 | tf_op jit(solution)/shard_map/ppermute | solution.py:351
  5.1 5.5 %collective-permute-start.1 = (bf16[128,256]{1,0:T(8,128)(2,1)S(1)}, bf16[128,256]{1,0:T(8,128)(2,1)S(1)}, u32[]{:S(2)}, u32[]{:S(2)}) collective-permute-start(bf16[128,256]{1,0:T(8,128)(2,1)S(1)} %get-tuple-element.61), channel_id=1, source_target_pairs={{0,6},{4,7},{8,3},{12,2},{1,14},{5,15},{9,11},{13,10},{2,4},{6,5},... | collective-permute-start | bytes 196616 | tf_op jit(solution)/shard_map/ppermute | solution.py:352
  10.7 1.1 broadcast_select_fusion.2
  11.8 1.9 %collective-permute-start.2 = (bf16[128,896]{1,0:T(8,128)(2,1)S(1)}, bf16[128,896]{1,0:T(8,128)(2,1)S(1)}, u32[]{:S(2)}, u32[]{:S(2)}) collective-permute-start(bf16[128,896]{1,0:T(8,128)(2,1)S(1)} %get-tuple-element.60), channel_id=1, source_target_pairs={{0,2},{4,3},{8,7},{12,6},{1,10},{5,11},{9,15},{13,14},{2,0},{6,1},... | collective-permute-start | bytes 688136 | tf_op jit(solution)/shard_map/ppermute | solution.py:351
  13.7 8.5 %collective-permute-start.3 = (bf16[128,896]{1,0:T(8,128)(2,1)S(1)}, bf16[128,896]{1,0:T(8,128)(2,1)S(1)}, u32[]{:S(2)}, u32[]{:S(2)}) collective-permute-start(bf16[128,896]{1,0:T(8,128)(2,1)S(1)} %get-tuple-element.59), channel_id=1, source_target_pairs={{0,6},{4,7},{8,3},{12,2},{1,14},{5,15},{9,11},{13,10},{2,4},{6,5},... | collective-permute-start | bytes 688136 | tf_op jit(solution)/shard_map/ppermute | solution.py:352
  22.4 0.8 negate_select_fusion
  23.9 13.8 %all_gather.3.refs_0_ = bf16[512,512]{1,0:T(8,128)(2,1)S(1)} all-gather(bf16[128,512]{1,0:T(8,128)(2,1)S(1)} %turn_keys.1), channel_id=1, replica_groups={{0,16,32,48},{64,80,96,112},{128,144,160,176},{192,208,224,240},{256,27..., dimensions={0}, use_global_device_ids=true | all-gather | bytes 655360 | tf_op jit(solution)/shard_map/all_gather | solution.py:369
  37.8 1.9 %collective-permute-start.4 = (bf16[2,128,896]{2,1,0:T(8,128)(2,1)S(1)}, bf16[2,128,896]{2,1,0:T(8,128)(2,1)S(1)}, u32[]{:S(2)}, u32[]{:S(2)}) collective-permute-start(bf16[2,128,896]{2,1,0:T(8,128)(2,1)S(1)} %pad_maximum_fusion.own_ref), channel_id=1, source_target_pairs={{0,1},{1,0},{2,3},{3,2},{4,5},{5,4},{6,7},{7,6},{8,9},{9,8},{10,11... | collective-permute-start | bytes 1376264 | tf_op jit(solution)/shard_map/ppermute | solution.py:373
  39.7 3.3 %collective-permute-start.7 = (bf16[512,512]{1,0:T(8,128)(2,1)S(1)}, bf16[512,512]{1,0:T(8,128)(2,1)S(1)}, u32[]{:S(2)}, u32[]{:S(2)}) collective-permute-start(bf16[512,512]{1,0:T(8,128)(2,1)S(1)} %all_gather.3.refs_0_), channel_id=1, source_target_pairs={{0,448},{1,449},{2,450},{3,451},{4,452},{5,453},{6,454},{7,455},{8... | collective-permute-start | bytes 1572872 | tf_op jit(solution)/shard_map/ppermute | solution.py:59
  43.0 3.8 %collective-permute-start.5 = (bf16[512,512]{1,0:T(8,128)(2,1)S(1)}, bf16[512,512]{1,0:T(8,128)(2,1)S(1)}, u32[]{:S(2)}, u32[]{:S(2)}) collective-permute-start(bf16[512,512]{1,0:T(8,128)(2,1)S(1)} %all_gather.3.refs_0_), channel_id=1, source_target_pairs={{0,64},{1,65},{2,66},{3,67},{4,68},{5,69},{6,70},{7,71},{8,72},{9,... | collective-permute-start | bytes 1572872 | tf_op jit(solution)/shard_map/ppermute | solution.py:59
  46.8 1.1 turn_queries.1.query_ref
  47.9 5.3 %attend.5 = (f32[4,896,128]{2,1,0:T(8,128)S(1)}, f32[4,896,128]{2,1,0:T(8,128)S(1)}, f32[4,896,128]{2,1,0:T(8,128)S(1)}) custom-call(s32[4]{0:T(128)S(1)} %pad_add_fusion.where_ref, bf16[5,896,128]{2,1,0:T(8,128)(2,1)S(1)} %turn_queries.1.query_ref, bf16[512,512]{1,0:T(8,128)(2,1)S(1)} %all_gather.3.refs_0_), custom_call_target="tpu_custom_call" | custom-call | flops 939524096 | bytes 4194304 | tf_op jit(solution)/shard_map/attend/pallas_call | solution.py:289
  53.2 3.9 %collective-permute-done.7.refs_1_ = bf16[512,512]{1,0:T(8,128)(2,1)S(1)} collective-permute-done((bf16[512,512]{1,0:T(8,128)(2,1)S(1)}, bf16[512,512]{1,0:T(8,128)(2,1)S(1)}, u32[]{:S(2)}, u32[]{:S(2)}) %collective-permute-start.7) | collective-permute-done | bytes 524320 | tf_op jit(solution)/shard_map/ppermute | solution.py:59
  57.1 2.0 %collective-permute-start.9 = (bf16[512,512]{1,0:T(8,128)(2,1)S(1)}, bf16[512,512]{1,0:T(8,128)(2,1)S(1)}, u32[]{:S(2)}, u32[]{:S(2)}) collective-permute-start(bf16[512,512]{1,0:T(8,128)(2,1)S(1)} %collective-permute-done.7.refs_1_), channel_id=1, source_target_pairs={{0,448},{1,449},{2,450},{3,451},{4,452},{5,453},{6,454},{7,455},{8... | collective-permute-start | bytes 1572872 | tf_op jit(solution)/shard_map/ppermute | solution.py:59
  59.2 5.0 %collective-permute-start.6 = (bf16[512,512]{1,0:T(8,128)(2,1)S(1)}, bf16[512,512]{1,0:T(8,128)(2,1)S(1)}, u32[]{:S(2)}, u32[]{:S(2)}) collective-permute-start(bf16[512,512]{1,0:T(8,128)(2,1)S(1)} %collective-permute-done.5.refs_0_), channel_id=1, source_target_pairs={{0,64},{1,65},{2,66},{3,67},{4,68},{5,69},{6,70},{7,71},{8,72},{9,... | collective-permute-start | bytes 1572872 | tf_op jit(solution)/shard_map/ppermute | solution.py:59
  64.2 9.2 %attend.6 = (f32[4,896,128]{2,1,0:T(8,128)S(1)}, f32[4,896,128]{2,1,0:T(8,128)S(1)}, f32[4,896,128]{2,1,0:T(8,128)S(1)}) custom-call(s32[4]{0:T(128)S(1)} %pad_add_fusion.where_ref, bf16[5,896,128]{2,1,0:T(8,128)(2,1)S(1)} %turn_queries.1.query_ref, bf16[512,512]{1,0:T(8,128)(2,1)S(1)} %collective-permute-done.5.refs_0_, ...), custom_call_target="tpu_custom_call" | custom-call | flops 1879048192 | bytes 4194304 | tf_op jit(solution)/shard_map/attend/pallas_call | solution.py:289
  73.7 1.9 %collective-permute-start.10 = (bf16[512,512]{1,0:T(8,128)(2,1)S(1)}, bf16[512,512]{1,0:T(8,128)(2,1)S(1)}, u32[]{:S(2)}, u32[]{:S(2)}) collective-permute-start(bf16[512,512]{1,0:T(8,128)(2,1)S(1)} %collective-permute-done.9.refs_1_), channel_id=1, source_target_pairs={{0,448},{1,449},{2,450},{3,451},{4,452},{5,453},{6,454},{7,455},{8... | collective-permute-start | bytes 1572872 | tf_op jit(solution)/shard_map/ppermute | solution.py:59
  75.6 5.1 %collective-permute-start.8 = (bf16[512,512]{1,0:T(8,128)(2,1)S(1)}, bf16[512,512]{1,0:T(8,128)(2,1)S(1)}, u32[]{:S(2)}, u32[]{:S(2)}) collective-permute-start(bf16[512,512]{1,0:T(8,128)(2,1)S(1)} %collective-permute-done.6.refs_0_), channel_id=1, source_target_pairs={{0,64},{1,65},{2,66},{3,67},{4,68},{5,69},{6,70},{7,71},{8,72},{9,... | collective-permute-start | bytes 1572872 | tf_op jit(solution)/shard_map/ppermute | solution.py:59
  80.8 9.0 %attend.7 = (f32[4,896,128]{2,1,0:T(8,128)S(1)}, f32[4,896,128]{2,1,0:T(8,128)S(1)}, f32[4,896,128]{2,1,0:T(8,128)S(1)}) custom-call(s32[4]{0:T(128)S(1)} %pad_add_fusion.where_ref, bf16[5,896,128]{2,1,0:T(8,128)(2,1)S(1)} %turn_queries.1.query_ref, bf16[512,512]{1,0:T(8,128)(2,1)S(1)} %collective-permute-done.6.refs_0_, ...), custom_call_target="tpu_custom_call" | custom-call | flops 1879048192 | bytes 4194304 | tf_op jit(solution)/shard_map/attend/pallas_call | solution.py:289
  89.8 1.9 %collective-permute-start.12 = (bf16[256,512]{1,0:T(8,128)(2,1)S(1)}, bf16[256,512]{1,0:T(8,128)(2,1)S(1)}, u32[]{:S(2)}, u32[]{:S(2)}) collective-permute-start(bf16[256,512]{1,0:T(8,128)(2,1)S(1)} %slice.41), channel_id=1, source_target_pairs={{0,448},{1,449},{2,450},{3,451},{4,452},{5,453},{6,454},{7,455},{8... | collective-permute-start | bytes 786440 | tf_op jit(solution)/shard_map/ppermute | solution.py:59
  91.8 5.4 %collective-permute-start.11 = (bf16[256,512]{1,0:T(8,128)(2,1)S(1)}, bf16[256,512]{1,0:T(8,128)(2,1)S(1)}, u32[]{:S(2)}, u32[]{:S(2)}) collective-permute-start(bf16[256,512]{1,0:T(8,128)(2,1)S(1)} %slice.40), channel_id=1, source_target_pairs={{0,64},{1,65},{2,66},{3,67},{4,68},{5,69},{6,70},{7,71},{8,72},{9,... | collective-permute-start | bytes 786440 | tf_op jit(solution)/shard_map/ppermute | solution.py:59
  97.1 5.3 %attend.8 = (f32[4,896,128]{2,1,0:T(8,128)S(1)}, f32[4,896,128]{2,1,0:T(8,128)S(1)}, f32[4,896,128]{2,1,0:T(8,128)S(1)}) custom-call(s32[4]{0:T(128)S(1)} %pad_add_fusion.where_ref, bf16[5,896,128]{2,1,0:T(8,128)(2,1)S(1)} %turn_queries.1.query_ref, bf16[512,512]{1,0:T(8,128)(2,1)S(1)} %collective-permute-done.8.refs_0_, ...), custom_call_target="tpu_custom_call" | custom-call | flops 1879048192 | bytes 4194304 | tf_op jit(solution)/shard_map/attend/pallas_call | solution.py:289
  102.5 3.5 %attend.9 = (f32[2,896,128]{2,1,0:T(8,128)S(1)}, f32[2,896,128]{2,1,0:T(8,128)S(1)}, f32[2,896,128]{2,1,0:T(8,128)S(1)}, f32[2,896,256]{2,1,0:T(8,128)S(1)}) custom-call(s32[4]{0:T(128)S(1)} %pad_add_fusion.where_ref, bf16[5,896,128]{2,1,0:T(8,128)(2,1)S(1)} %turn_queries.1.query_ref, bf16[256,512]{1,0:T(8,128)(2,1)S(1)} %collective-permute-done.11.refs_0_.refs_2_, ...), custom_call_target="tpu_custom_call" | custom-call | flops 1879048192 | bytes 4194304 | tf_op jit(solution)/shard_map/attend/pallas_call | solution.py:289
  106.0 1.9 %collective-permute-start.13 = (f32[2,896,256]{2,1,0:T(8,128)S(1)}, f32[2,896,256]{2,1,0:T(8,128)S(1)}, u32[]{:S(2)}, u32[]{:S(2)}) collective-permute-start(f32[2,896,256]{2,1,0:T(8,128)S(1)} %get-tuple-element.54), channel_id=1, source_target_pairs={{0,1},{1,0},{2,3},{3,2},{4,5},{5,4},{6,7},{7,6},{8,9},{9,8},{10,11... | collective-permute-start | bytes 5505032 | tf_op jit(solution)/shard_map/ppermute | solution.py:412
  107.9 6.2 %rest.1.own_ref = f32[2,896,256]{2,1,0:T(8,128)S(1)} custom-call(s32[4]{0:T(128)S(1)} %pad_add_fusion.where_ref, bf16[5,896,128]{2,1,0:T(8,128)(2,1)S(1)} %turn_queries.1.query_ref, bf16[512,512]{1,0:T(8,128)(2,1)S(1)} %collective-permute-done.8.refs_0_, bf16[512,512]{1,0:T(8,128)(2,1)S(1)} %collective-permute-done.10.refs_1_, ...), custom_call_target="tpu_custom_call" | custom-call | flops 704643072 | bytes 4194304 | tf_op jit(solution)/shard_map/rest/pallas_call | solution.py:267
  114.1 1.3 merge.1
  115.4 1.9 %collective-permute-start.14 = (bf16[128,896]{1,0:T(8,128)(2,1)S(1)}, bf16[128,896]{1,0:T(8,128)(2,1)S(1)}, u32[]{:S(2)}, u32[]{:S(2)}) collective-permute-start(bf16[128,896]{1,0:T(8,128)(2,1)S(1)} %get-tuple-element.57), channel_id=1, source_target_pairs={{2,0},{3,4},{7,8},{6,12},{10,1},{11,5},{15,9},{14,13},{0,2},{1,6},... | collective-permute-start | bytes 688136 | tf_op jit(solution)/shard_map/ppermute | solution.py:422
  117.4 3.6 %collective-permute-start.15 = (bf16[128,896]{1,0:T(8,128)(2,1)S(1)}, bf16[128,896]{1,0:T(8,128)(2,1)S(1)}, u32[]{:S(2)}, u32[]{:S(2)}) collective-permute-start(bf16[128,896]{1,0:T(8,128)(2,1)S(1)} %get-tuple-element.58), channel_id=1, source_target_pairs={{6,0},{7,4},{3,8},{2,12},{14,1},{15,5},{11,9},{10,13},{4,2},{5,6},... | collective-permute-start | bytes 688136 | tf_op jit(solution)/shard_map/ppermute | solution.py:423
  121.0 4.7 %collective-permute-done.14 = bf16[128,896]{1,0:T(8,128)(2,1)S(1)} collective-permute-done((bf16[128,896]{1,0:T(8,128)(2,1)S(1)}, bf16[128,896]{1,0:T(8,128)(2,1)S(1)}, u32[]{:S(2)}, u32[]{:S(2)}) %collective-permute-start.14) | collective-permute-done | bytes 229408 | tf_op jit(solution)/shard_map/ppermute | solution.py:422
  125.7 8.3 %collective-permute-done.15 = bf16[128,896]{1,0:T(8,128)(2,1)S(1)} collective-permute-done((bf16[128,896]{1,0:T(8,128)(2,1)S(1)}, bf16[128,896]{1,0:T(8,128)(2,1)S(1)}, u32[]{:S(2)}, u32[]{:S(2)}) %collective-permute-start.15) | collective-permute-done | bytes 229408 | tf_op jit(solution)/shard_map/ppermute | solution.py:423
  134.1 0.8 pad_maximum_fusion.1
  (27 shorter events, 1.4 us)
Async XLA Ops:
  0.9 22.4 %collective-permute-start = (bf16[128,256]{1,0:T(8,128)(2,1)S(1)}, bf16[128,256]{1,0:T(8,128)(2,1)S(1)}, u32[]{:S(2)}, u32[]{:S(2)}) collective-permute-start(bf16[128,256]{1,0:T(8,128)(2,1)S(1)} %get-tuple-element.62), channel_id=1, source_target_pairs={{0,2},{4,3},{8,7},{12,6},{1,10},{5,11},{9,15},{13,14},{2,0},{6,1},... | collective-permute-start | bytes 196616 | tf_op jit(solution)/shard_map/ppermute | solution.py:351
  5.1 18.2 %collective-permute-start.1 = (bf16[128,256]{1,0:T(8,128)(2,1)S(1)}, bf16[128,256]{1,0:T(8,128)(2,1)S(1)}, u32[]{:S(2)}, u32[]{:S(2)}) collective-permute-start(bf16[128,256]{1,0:T(8,128)(2,1)S(1)} %get-tuple-element.61), channel_id=1, source_target_pairs={{0,6},{4,7},{8,3},{12,2},{1,14},{5,15},{9,11},{13,10},{2,4},{6,5},... | collective-permute-start | bytes 196616 | tf_op jit(solution)/shard_map/ppermute | solution.py:352
  11.8 25.9 %collective-permute-start.2 = (bf16[128,896]{1,0:T(8,128)(2,1)S(1)}, bf16[128,896]{1,0:T(8,128)(2,1)S(1)}, u32[]{:S(2)}, u32[]{:S(2)}) collective-permute-start(bf16[128,896]{1,0:T(8,128)(2,1)S(1)} %get-tuple-element.60), channel_id=1, source_target_pairs={{0,2},{4,3},{8,7},{12,6},{1,10},{5,11},{9,15},{13,14},{2,0},{6,1},... | collective-permute-start | bytes 688136 | tf_op jit(solution)/shard_map/ppermute | solution.py:351
  13.7 24.0 %collective-permute-start.3 = (bf16[128,896]{1,0:T(8,128)(2,1)S(1)}, bf16[128,896]{1,0:T(8,128)(2,1)S(1)}, u32[]{:S(2)}, u32[]{:S(2)}) collective-permute-start(bf16[128,896]{1,0:T(8,128)(2,1)S(1)} %get-tuple-element.59), channel_id=1, source_target_pairs={{0,6},{4,7},{8,3},{12,2},{1,14},{5,15},{9,11},{13,10},{2,4},{6,5},... | collective-permute-start | bytes 688136 | tf_op jit(solution)/shard_map/ppermute | solution.py:352
  37.8 9.0 %collective-permute-start.4 = (bf16[2,128,896]{2,1,0:T(8,128)(2,1)S(1)}, bf16[2,128,896]{2,1,0:T(8,128)(2,1)S(1)}, u32[]{:S(2)}, u32[]{:S(2)}) collective-permute-start(bf16[2,128,896]{2,1,0:T(8,128)(2,1)S(1)} %pad_maximum_fusion.own_ref), channel_id=1, source_target_pairs={{0,1},{1,0},{2,3},{3,2},{4,5},{5,4},{6,7},{7,6},{8,9},{9,8},{10,11... | collective-permute-start | bytes 1376264 | tf_op jit(solution)/shard_map/ppermute | solution.py:373
  39.7 17.4 %collective-permute-start.7 = (bf16[512,512]{1,0:T(8,128)(2,1)S(1)}, bf16[512,512]{1,0:T(8,128)(2,1)S(1)}, u32[]{:S(2)}, u32[]{:S(2)}) collective-permute-start(bf16[512,512]{1,0:T(8,128)(2,1)S(1)} %all_gather.3.refs_0_), channel_id=1, source_target_pairs={{0,448},{1,449},{2,450},{3,451},{4,452},{5,453},{6,454},{7,455},{8... | collective-permute-start | bytes 1572872 | tf_op jit(solution)/shard_map/ppermute | solution.py:59
  43.0 16.2 %collective-permute-start.5 = (bf16[512,512]{1,0:T(8,128)(2,1)S(1)}, bf16[512,512]{1,0:T(8,128)(2,1)S(1)}, u32[]{:S(2)}, u32[]{:S(2)}) collective-permute-start(bf16[512,512]{1,0:T(8,128)(2,1)S(1)} %all_gather.3.refs_0_), channel_id=1, source_target_pairs={{0,64},{1,65},{2,66},{3,67},{4,68},{5,69},{6,70},{7,71},{8,72},{9,... | collective-permute-start | bytes 1572872 | tf_op jit(solution)/shard_map/ppermute | solution.py:59
  57.1 16.6 %collective-permute-start.9 = (bf16[512,512]{1,0:T(8,128)(2,1)S(1)}, bf16[512,512]{1,0:T(8,128)(2,1)S(1)}, u32[]{:S(2)}, u32[]{:S(2)}) collective-permute-start(bf16[512,512]{1,0:T(8,128)(2,1)S(1)} %collective-permute-done.7.refs_1_), channel_id=1, source_target_pairs={{0,448},{1,449},{2,450},{3,451},{4,452},{5,453},{6,454},{7,455},{8... | collective-permute-start | bytes 1572872 | tf_op jit(solution)/shard_map/ppermute | solution.py:59
  59.2 16.4 %collective-permute-start.6 = (bf16[512,512]{1,0:T(8,128)(2,1)S(1)}, bf16[512,512]{1,0:T(8,128)(2,1)S(1)}, u32[]{:S(2)}, u32[]{:S(2)}) collective-permute-start(bf16[512,512]{1,0:T(8,128)(2,1)S(1)} %collective-permute-done.5.refs_0_), channel_id=1, source_target_pairs={{0,64},{1,65},{2,66},{3,67},{4,68},{5,69},{6,70},{7,71},{8,72},{9,... | collective-permute-start | bytes 1572872 | tf_op jit(solution)/shard_map/ppermute | solution.py:59
  73.7 16.1 %collective-permute-start.10 = (bf16[512,512]{1,0:T(8,128)(2,1)S(1)}, bf16[512,512]{1,0:T(8,128)(2,1)S(1)}, u32[]{:S(2)}, u32[]{:S(2)}) collective-permute-start(bf16[512,512]{1,0:T(8,128)(2,1)S(1)} %collective-permute-done.9.refs_1_), channel_id=1, source_target_pairs={{0,448},{1,449},{2,450},{3,451},{4,452},{5,453},{6,454},{7,455},{8... | collective-permute-start | bytes 1572872 | tf_op jit(solution)/shard_map/ppermute | solution.py:59
  75.6 16.1 %collective-permute-start.8 = (bf16[512,512]{1,0:T(8,128)(2,1)S(1)}, bf16[512,512]{1,0:T(8,128)(2,1)S(1)}, u32[]{:S(2)}, u32[]{:S(2)}) collective-permute-start(bf16[512,512]{1,0:T(8,128)(2,1)S(1)} %collective-permute-done.6.refs_0_), channel_id=1, source_target_pairs={{0,64},{1,65},{2,66},{3,67},{4,68},{5,69},{6,70},{7,71},{8,72},{9,... | collective-permute-start | bytes 1572872 | tf_op jit(solution)/shard_map/ppermute | solution.py:59
  89.8 12.7 %collective-permute-start.12 = (bf16[256,512]{1,0:T(8,128)(2,1)S(1)}, bf16[256,512]{1,0:T(8,128)(2,1)S(1)}, u32[]{:S(2)}, u32[]{:S(2)}) collective-permute-start(bf16[256,512]{1,0:T(8,128)(2,1)S(1)} %slice.41), channel_id=1, source_target_pairs={{0,448},{1,449},{2,450},{3,451},{4,452},{5,453},{6,454},{7,455},{8... | collective-permute-start | bytes 786440 | tf_op jit(solution)/shard_map/ppermute | solution.py:59
  91.8 10.7 %collective-permute-start.11 = (bf16[256,512]{1,0:T(8,128)(2,1)S(1)}, bf16[256,512]{1,0:T(8,128)(2,1)S(1)}, u32[]{:S(2)}, u32[]{:S(2)}) collective-permute-start(bf16[256,512]{1,0:T(8,128)(2,1)S(1)} %slice.40), channel_id=1, source_target_pairs={{0,64},{1,65},{2,66},{3,67},{4,68},{5,69},{6,70},{7,71},{8,72},{9,... | collective-permute-start | bytes 786440 | tf_op jit(solution)/shard_map/ppermute | solution.py:59
  106.0 8.1 %collective-permute-start.13 = (f32[2,896,256]{2,1,0:T(8,128)S(1)}, f32[2,896,256]{2,1,0:T(8,128)S(1)}, u32[]{:S(2)}, u32[]{:S(2)}) collective-permute-start(f32[2,896,256]{2,1,0:T(8,128)S(1)} %get-tuple-element.54), channel_id=1, source_target_pairs={{0,1},{1,0},{2,3},{3,2},{4,5},{5,4},{6,7},{7,6},{8,9},{9,8},{10,11... | collective-permute-start | bytes 5505032 | tf_op jit(solution)/shard_map/ppermute | solution.py:412
  115.4 10.2 %collective-permute-start.14 = (bf16[128,896]{1,0:T(8,128)(2,1)S(1)}, bf16[128,896]{1,0:T(8,128)(2,1)S(1)}, u32[]{:S(2)}, u32[]{:S(2)}) collective-permute-start(bf16[128,896]{1,0:T(8,128)(2,1)S(1)} %get-tuple-element.57), channel_id=1, source_target_pairs={{2,0},{3,4},{7,8},{6,12},{10,1},{11,5},{15,9},{14,13},{0,2},{1,6},... | collective-permute-start | bytes 688136 | tf_op jit(solution)/shard_map/ppermute | solution.py:422
  117.4 16.7 %collective-permute-start.15 = (bf16[128,896]{1,0:T(8,128)(2,1)S(1)}, bf16[128,896]{1,0:T(8,128)(2,1)S(1)}, u32[]{:S(2)}, u32[]{:S(2)}) collective-permute-start(bf16[128,896]{1,0:T(8,128)(2,1)S(1)} %get-tuple-element.58), channel_id=1, source_target_pairs={{6,0},{7,4},{3,8},{2,12},{14,1},{15,5},{11,9},{10,13},{4,2},{5,6},... | collective-permute-start | bytes 688136 | tf_op jit(solution)/shard_map/ppermute | solution.py:423
